TPU v7x, 128 devices: a whole 4x4x4 slice. The times are simulated.
128 devices in a mesh: row: 16 (over z, x), col: 8 (over y, core).
Axes of the slice: x: 4, y: 4, z: 4, core: 2. Of those that a mesh axis runs over, the one named last changes fastest.
Arguments:
- amplitudes: float32 [192, 10, 10, 2048], P('row', None, None, 'col'), may hold values from -6 to 6
- old_blocks: int32 [16, 12], replicated, may hold values from 0 to 135, as said below
- old_counts: int32 [16], replicated, may hold values from 1 to 12, as said below
- new_phase: int32 [1], replicated, may hold values from 0 to 15
- fock: float32 [160, 160], P('row'), may hold values from -0.5 to 0.5
Outputs:
- contracted: float32 [16, 10, 160, 2048], P('row', None, None, 'col')
Inputs may be any that keep to these rules, and one draw needn't show every extreme that they name: `old_blocks`: over the live slots of all row devices every tile pair id 0 to 135 stands exactly once; ids in slots that are not live are arbitrary. For every residue r mod 16, at most 3 live blocks of one row device hold a tile whose index is r mod 16, and some device reaches 3 for some r. `old_counts`: the counts sum to 136; some device has exactly 12.
All inputs are finite; a program needn't handle non-finite values.
Results may differ from a plain program's by a relative error of at most 0.00007.
Values sent between devices are 32-bit elements; how exact they have to be, the bound alone decides.
A program may use at most 128 MiB of HBM per device.

v0:
```python
import jax
import jax.numpy as jnp
import numpy as np
from jax import lax
from jax.sharding import PartitionSpec as P

NT = 16


def joined_along(parts, dim):
    parts = jnp.moveaxis(parts, 0, dim)
    shape = parts.shape
    return parts.reshape(*shape[:dim], shape[dim] * shape[dim + 1], *shape[dim + 2 :])


def copy_for_each(array, axis):
    devices = lax.axis_size(axis)
    return lax.all_to_all(
        jnp.broadcast_to(array[None], (devices, *array.shape)), axis, 0, 0, tiled=True
    )


def collect(array, axis, dim):
    return joined_along(copy_for_each(array, axis), dim)


def in_blocks(array, dim, devices):
    shape = array.shape
    parts = array.reshape(*shape[:dim], devices, shape[dim] // devices, *shape[dim + 1 :])
    return jnp.moveaxis(parts, dim, 0)


def piece_ends(length, count):
    hop = length // count
    if hop >= 8:
        hop -= hop % 8
    return [hop * k for k in range(1, count)]


def several_exchanges(array, axis, pieces, split_dim, concat_dim):
    parts = in_blocks(array, split_dim, lax.axis_size(axis))
    split_at = max(range(1, max(2, parts.ndim - 1)), key=lambda d: parts.shape[d])
    finished = []
    for piece in jnp.split(parts, piece_ends(parts.shape[split_at], pieces), axis=split_at):
        if piece.size:
            finished.append(lax.all_to_all(piece, axis, split_axis=0, concat_axis=0, tiled=True))
    return joined_along(jnp.concatenate(finished, axis=split_at), concat_dim)


def pair_table():
    table = np.zeros((NT, NT), np.int32)
    first_tile = np.zeros((NT * (NT + 1) // 2,), np.int32)
    second_tile = np.zeros((NT * (NT + 1) // 2,), np.int32)
    for first in range(NT):
        for second in range(NT):
            low = min(first, second)
            high = max(first, second)
            ident = low * NT - low * (low - 1) // 2 + (high - low)
            table[first, second] = ident
            first_tile[ident] = low
            second_tile[ident] = high
    return (table, first_tile, second_tile)


def body(amplitudes, old_blocks, old_counts, new_phase, fock):
    nrows = lax.axis_size("row")
    myself = lax.axis_index("row")
    slots = amplitudes.shape[0]
    tile = amplitudes.shape[1]
    occ_dev = amplitudes.shape[3]
    width = fock.shape[1]
    per_dev = NT // nrows
    nblocks = NT * (NT + 1) // 2
    phase = new_phase[0]
    table, first_tile, second_tile = pair_table()
    live = jnp.arange(slots, dtype=jnp.int32)[None, :] < old_counts[:, None]
    flat = amplitudes.reshape(slots, tile * tile * occ_dev)
    fock_full = collect(fock, "row", 0)
    match_ids = old_blocks.reshape(-1)
    match_live = live.reshape(-1)
    my_ids = lax.dynamic_slice_in_dim(old_blocks, myself, 1, 0)[0]
    my_live = lax.dynamic_slice_in_dim(live, myself, 1, 0)[0]
    owner_low = (jnp.asarray(first_tile)[my_ids] + phase) % nrows
    owner_high = (jnp.asarray(second_tile)[my_ids] + phase) % nrows
    target = jnp.arange(nrows, dtype=jnp.int32)[:, None]
    sending = ((owner_low[None, :] == target) | (owner_high[None, :] == target)) & my_live[None, :]
    capacity = per_dev * ((slots - 2) // 8 + 2)
    ordinal = jnp.cumsum(sending.astype(jnp.int32), axis=1) - 1
    packing = (
        ordinal[:, None, :] == jnp.arange(capacity, dtype=jnp.int32)[None, :, None]
    ) & sending[:, None, :]
    payload = jnp.einsum(
        "dcs,sp->dcp", packing.astype(jnp.float32), flat, precision=lax.Precision.HIGHEST
    )
    filled = jnp.any(packing, axis=2)
    sent_ids = jnp.sum(jnp.where(packing, my_ids[None, None, :], 0), axis=2)
    sent_ids = jnp.where(filled, sent_ids, nblocks)
    payload_in, ids_in = (
        several_exchanges(payload, "row", 2, 0, 0),
        several_exchanges(sent_ids, "row", 2, 0, 0),
    )
    received = payload_in
    match_ids = ids_in.reshape(-1)
    match_live = match_ids < nblocks
    received = received.reshape(-1, tile * tile * occ_dev)
    index = jnp.arange(tile, dtype=jnp.int32)
    column_tile = (myself - phase) % nrows + 0
    needed = jnp.asarray(table)[:, column_tile]
    picker = ((match_ids[None, :] == needed[:, None]) & match_live[None, :]).astype(jnp.float32)
    chosen = jnp.dot(picker, received, precision=lax.Precision.HIGHEST)
    chosen = chosen.reshape(NT, tile, tile, occ_dev)
    c_global = jnp.arange(NT, dtype=jnp.int32)[:, None, None] * tile + index[None, :, None]
    b_global = column_tile * tile + index[None, None, :]
    below = (c_global < b_global)[:, :, :, None]
    above = (c_global > b_global)[:, :, :, None]
    dense = jnp.where(below, chosen, jnp.where(above, -jnp.swapaxes(chosen, 1, 2), 0.0))
    dense = dense.reshape(width, tile, occ_dev)
    outcome = jnp.einsum("ac,cbj->baj", fock_full, dense, precision=lax.Precision.HIGHEST)
    results = [outcome]
    return jnp.stack(results, 0)


def solution(mesh):
    return jax.shard_map(
        body,
        mesh=mesh,
        in_specs=(P("row", None, None, "col"), P(), P(), P(), P("row", None)),
        out_specs=P("row", None, None, "col"),
        check_vma=False,
    )
```

profile of v0, /device:TPU:0, one launch (start us, length us, event | category | flops | bytes accessed | tf_op | source)
XLA Modules:
  0.0 153.7 jit_solution(27221250727924344)
XLA Ops:
  0.0 0.7 fusion.18
  0.7 0.7 fusion.19
  1.4 1.3 gather_fusion
  2.7 1.3 gather_fusion.1
  4.7 1.2 dynamic-slice
  7.9 8.0 %all-to-all-start = ((s32[16,1,3]{2,1,0:T(1,128)}), s32[16,1,3]{2,1,0:T(1,128)S(1)}, u32[]{:S(2)}, u32[]{:S(2)}) async-start(s32[16,1,3]{2,1,0:T(1,128)} %copy.17), calls=%async_computation | async-start | bytes 16384 | tf_op jit(solution)/shard_map/all_to_all | solution.py:46
  15.8 2.2 %copy.18 = f32[12,10,10,256]{3,2,1,0:T(8,128)S(1)} copy(f32[12,10,10,256]{3,0,2,1:T(8,128)} %param.8) | data formatting | bytes 2457600 | tf_op args[0]
  18.1 1.5 reshape.242
  19.5 0.9 reshape.256
  20.4 3.0 %all-to-all-done = s32[16,1,3]{2,1,0:T(1,128)S(1)} async-done(((s32[16,1,3]{2,1,0:T(1,128)}), s32[16,1,3]{2,1,0:T(1,128)S(1)}, u32[]{:S(2)}, u32[]{:S(2)}) %all-to-all-start) | async-done | bytes 224 | tf_op jit(solution)/shard_map/all_to_all | solution.py:46
  23.4 4.2 %all-to-all-start.3 = ((f32[16,1,1600]{2,1,0:T(1,128)}), f32[16,1,1600]{2,1,0:T(1,128)S(1)}, u32[]{:S(2)}, u32[]{:S(2)}) async-start(f32[16,1,1600]{2,1,0:T(1,128)} %reshape.256), calls=%async_computation.3 | async-start | bytes 212992 | tf_op jit(solution)/shard_map/all_to_all | solution.py:18
  27.6 3.5 %convolution_bitcast_fusion = f32[16,1,3,25600]{3,0,2,1:T(8,128)S(1)} fusion(f32[12,25600,1]{1,0,2:T(8,128)} %reshape.242, s32[16,12]{1,0:T(8,128)S(1)} %broadcast_add_fusion, pred[16,12]{1,0:T(8,128)(4,1)S(1)} %get-tuple-element.7), kind=kOutput, calls=%fused_computation.2 | convolution fusion | flops 176948352 | bytes 6144960 | tf_op jit(solution)/shard_map/dcs,sp->dcp/dot_general | solution.py:92
  31.2 2.2 %copy-done = f32[16,1,3,25600]{3,0,2,1:T(8,128)} copy-done((f32[16,1,3,25600]{3,0,2,1:T(8,128)}, f32[16,1,3,25600]{3,0,2,1:T(8,128)S(1)}, u32[]{:S(2)}) %copy-start) | copy-done | bytes 4915224
  33.5 2.8 %copy.19 = f32[16,1,1,25600]{3,2,1,0:T(1,128)} copy(f32[16,1,1,25600]{3,0,2,1:T(8,128)S(1)} %split.8) | data formatting | bytes 3276800 | tf_op jit(solution)/shard_map/split | solution.py:44
  36.3 7.2 %all-to-all-start.1 = ((f32[16,1,1,25600]{3,2,1,0:T(1,128)}), f32[16,1,1,25600]{3,2,1,0:T(1,128)S(1)}, u32[]{:S(2)}, u32[]{:S(2)}) async-start(f32[16,1,1,25600]{3,2,1,0:T(1,128)} %copy.19), calls=%async_computation.1 | async-start | bytes 3276800 | tf_op jit(solution)/shard_map/all_to_all | solution.py:46
  43.6 1.9 %slice-done = f32[16,1,2,25600]{3,0,2,1:T(8,128)S(1)} async-done(((f32[16,1,3,25600]{3,0,2,1:T(8,128)}), f32[16,1,2,25600]{3,0,2,1:T(8,128)S(1)}, s32[]{:S(2)}) %slice-start) | async-done | bytes 3276824 | tf_op jit(solution)/shard_map/split | solution.py:44
  45.5 4.2 %copy.20 = f32[16,1,2,25600]{3,2,1,0:T(2,128)} copy(f32[16,1,2,25600]{3,0,2,1:T(8,128)S(1)} %slice-done) | data formatting | bytes 6553600 | tf_op jit(solution)/shard_map/split | solution.py:44
  49.7 17.1 %all-to-all-done.1 = f32[16,1,1,25600]{3,2,1,0:T(1,128)S(1)} async-done(((f32[16,1,1,25600]{3,2,1,0:T(1,128)}), f32[16,1,1,25600]{3,2,1,0:T(1,128)S(1)}, u32[]{:S(2)}, u32[]{:S(2)}) %all-to-all-start.1) | async-done | bytes 1638432 | tf_op jit(solution)/shard_map/all_to_all | solution.py:46
  66.7 1.2 copy-done.1
  67.9 3.9 %all-to-all-start.2 = ((f32[16,1,2,25600]{3,2,1,0:T(2,128)}), f32[16,1,2,25600]{3,2,1,0:T(2,128)S(1)}, u32[]{:S(2)}, u32[]{:S(2)}) async-start(f32[16,1,2,25600]{3,2,1,0:T(2,128)} %copy.20), calls=%async_computation.2 | async-start | bytes 6553600 | tf_op jit(solution)/shard_map/all_to_all | solution.py:46
  71.9 0.7 dynamic-slice_bitcast_fusion
  72.6 0.7 broadcast_compare_fusion.1
  75.1 1.4 reduce.4
  76.6 1.0 reshape.257
  78.3 40.8 %all-to-all-done.2 = f32[16,1,2,25600]{3,2,1,0:T(2,128)S(1)} async-done(((f32[16,1,2,25600]{3,2,1,0:T(2,128)}), f32[16,1,2,25600]{3,2,1,0:T(2,128)S(1)}, u32[]{:S(2)}, u32[]{:S(2)}) %all-to-all-start.2) | async-done | bytes 3276832 | tf_op jit(solution)/shard_map/all_to_all | solution.py:46
  119.1 7.1 %pad_maximum_fusion = f32[16,1,3,25600]{3,2,1,0:T(4,128)} fusion(f32[16,1,2,25600]{3,2,1,0:T(2,128)S(1)} %all-to-all-done.2, f32[16,1,1,25600]{3,2,1,0:T(1,128)} %copy-done.1), kind=kLoop, calls=%fused_computation.3 | loop fusion | flops 1228800 | bytes 9830400 | tf_op jit(solution)/shard_map/concatenate | solution.py:47
  126.2 5.8 %reshape_reshape.4 = f32[48,25600]{1,0:T(8,128)} reshape(f32[16,1,3,25600]{3,2,1,0:T(4,128)} %pad_maximum_fusion) | data formatting | bytes 9830400 | tf_op jit(solution)/shard_map/reshape;reshape | solution.py:105
  132.1 6.9 %dot_general.15 = f32[10,10,256,48]{2,1,0,3:T(8,128)} reshape(f32[25600,48]{0,1:T(8,128)} %bitcast.38) | data formatting | bytes 9830400 | tf_op jit(solution)/shard_map/dot_general | solution.py:110
  138.9 7.5 %fusion = f32[16,10,10,256]{3,0,2,1:T(8,128)S(1)} fusion(f32[10,10,256,48]{2,1,0,3:T(8,128)} %dot_general.15, s32[48]{0:T(128)S(1)} %eq.86, s32[16]{0:T(128)S(1)} %dynamic-slice_bitcast_fusion, pred[48]{0:T(512)(128)(4,1)S(1)} %broadcast_compare_fusion.2), kind=kOutput, calls=%fused_computation.4 | convolution fusion | flops 235931136 | bytes 6553904 | tf_op jit(solution)/shard_map/dot_general | solution.py:110
  147.1 1.1 copy.23
  148.2 1.3 reshape.224
  149.5 4.2 %convolution_bitcast_fusion.1 = f32[1,10,160,256]{3,2,1,0:T(8,128)} fusion(f32[160,10,256]{2,0,1:T(8,128)} %reshape.224, f32[160,160,1]{1,0,2:T(8,128)S(1)} %copy-done.2), kind=kOutput, calls=%fused_computation.9 | convolution fusion | flops 786432000 | bytes 3379200 | tf_op jit(solution)/shard_map/ac,cbj->baj/dot_general | solution.py:118
  (34 shorter events, 5.1 us)
Async XLA Ops:
  7.9 15.6 %all-to-all-start = ((s32[16,1,3]{2,1,0:T(1,128)}), s32[16,1,3]{2,1,0:T(1,128)S(1)}, u32[]{:S(2)}, u32[]{:S(2)}) async-start(s32[16,1,3]{2,1,0:T(1,128)} %copy.17), calls=%async_computation | async-start | bytes 16384 | tf_op jit(solution)/shard_map/all_to_all | solution.py:46
  18.0 1.5 copy-start.5
  23.4 12.9 %all-to-all-start.3 = ((f32[16,1,1600]{2,1,0:T(1,128)}), f32[16,1,1600]{2,1,0:T(1,128)S(1)}, u32[]{:S(2)}, u32[]{:S(2)}) async-start(f32[16,1,1600]{2,1,0:T(1,128)} %reshape.256), calls=%async_computation.3 | async-start | bytes 212992 | tf_op jit(solution)/shard_map/all_to_all | solution.py:18
  31.2 2.2 %copy-start = (f32[16,1,3,25600]{3,0,2,1:T(8,128)}, f32[16,1,3,25600]{3,0,2,1:T(8,128)S(1)}, u32[]{:S(2)}) copy-start(f32[16,1,3,25600]{3,0,2,1:T(8,128)S(1)} %convolution_bitcast_fusion) | copy-start | bytes 14745604
  36.3 30.4 %all-to-all-start.1 = ((f32[16,1,1,25600]{3,2,1,0:T(1,128)}), f32[16,1,1,25600]{3,2,1,0:T(1,128)S(1)}, u32[]{:S(2)}, u32[]{:S(2)}) async-start(f32[16,1,1,25600]{3,2,1,0:T(1,128)} %copy.19), calls=%async_computation.1 | async-start | bytes 3276800 | tf_op jit(solution)/shard_map/all_to_all | solution.py:46
  43.5 1.9 %slice-start = ((f32[16,1,3,25600]{3,0,2,1:T(8,128)}), f32[16,1,2,25600]{3,0,2,1:T(8,128)S(1)}, s32[]{:S(2)}) async-start(f32[16,1,3,25600]{3,0,2,1:T(8,128)} %copy-done), calls=%async_computation.4 | async-start | bytes 6553600 | tf_op jit(solution)/shard_map/split | solution.py:44
  66.7 1.2 copy-start.1
  67.9 51.2 %all-to-all-start.2 = ((f32[16,1,2,25600]{3,2,1,0:T(2,128)}), f32[16,1,2,25600]{3,2,1,0:T(2,128)S(1)}, u32[]{:S(2)}, u32[]{:S(2)}) async-start(f32[16,1,2,25600]{3,2,1,0:T(2,128)} %copy.20), calls=%async_computation.2 | async-start | bytes 6553600 | tf_op jit(solution)/shard_map/all_to_all | solution.py:46
  138.9 7.6 %copy-start.3 = (pred[16,10,10]{0,2,1:T(8,128)(4,1)S(1)}, pred[16,10,10]{0,2,1:T(8,128)(4,1)}, u32[]{:S(2)}) copy-start(pred[16,10,10]{0,2,1:T(8,128)(4,1)} %get-tuple-element.5) | copy-start | bytes 4804
  138.9 7.6 %copy-start.4 = (pred[16,10,10]{0,2,1:T(8,128)(4,1)S(1)}, pred[16,10,10]{0,2,1:T(8,128)(4,1)}, u32[]{:S(2)}) copy-start(pred[16,10,10]{0,2,1:T(8,128)(4,1)} %get-tuple-element.6) | copy-start | bytes 4804
  148.2 1.3 copy-start.2
where the time goes:
time: 155 us; the launch traced here: 154 us
  waiting for transfers between devices  60.9 us (39%)
  local copies, waits for them, and re-layouts  40.9 us (26%)
  starting transfers between devices  23.3 us (15%)
  matrix products  15.3 us (10%)
  other arithmetic  12.4 us (8%)
    all_to_all x3, waiting for transfers between devices, several_exchanges(): lax.all_to_all(piece, axis, split_axis=0, concat_axis=0, tiled=True)  60.9 us
    all_to_all x3, starting transfers between devices, several_exchanges(): lax.all_to_all(piece, axis, split_axis=0, concat_axis=0, tiled=True)  19.1 us
    split x5, local copies, waits for them, and re-layouts, several_exchanges(): jnp.split(parts, piece_ends(parts.shape[split_at], pieces), axis=split_at)  9.07 us
    dot_general x1, matrix products, body(): chosen = jnp.dot(picker, received, precision=lax.Precision.HIGHEST)  7.54 us
    unnamed x15, local copies, waits for them, and re-layouts  7.43 us
    concatenate x1, other arithmetic, several_exchanges(): return joined_along(jnp.concatenate(finished, axis=split_at), concat_dim)  7.12 us
    dot_general x1, local copies, waits for them, and re-layouts, body(): chosen = jnp.dot(picker, received, precision=lax.Precision.HIGHEST)  6.86 us
    another operation x1, local copies, waits for them, and re-layouts, body(): received = received.reshape(-1, tile * tile * occ_dev)  5.84 us
  transfers between devices with their start and end apart: 4, of which 3 were waited for; matrix products, arithmetic and copies ran while one was open for 14% of the time, Pallas kernels for 0%

commit v1 on v0

v1 whole, which is shorter than its diff:
```python
import jax
import jax.numpy as jnp
import numpy as np
from jax import lax
from jax.experimental import pallas as pl
from jax.experimental.pallas import tpu as pltpu
from jax.sharding import PartitionSpec as P

NT = 16
BT = 10
NR = 16
SLOTS = 12
PIECE = 13
SROWS = 160
CROWS = NT * PIECE
LANES = 128
TYPE_A = 10
MESH = pl.DeviceIdType.MESH


def piece_tables():
    pairs = [(x, y, h) for h in range(2) for x in range(BT) for y in range(x + 1, BT)]
    diagonal = [(x, x, h) for h in range(2) for x in range(BT)]
    pieces = []
    for m in range(NR):
        rows = []
        for _ in range(6 if m < TYPE_A else 5):
            x, y, h = pairs.pop(0)
            rows += [(x, y, h), (y, x, h)]
        for _ in range(1 if m < TYPE_A else 2):
            if diagonal:
                rows.append(diagonal.pop(0))
        pieces.append(rows)
    assert not pairs and not diagonal
    where = {row: (m, j) for m, rows in enumerate(pieces) for j, row in enumerate(rows)}
    return pieces, where


def kernel(
    table_ref, amp_hbm, fock_ref, out_hbm,
    amp, send1, recv1, send2, recv2, coef_a, coef_b, fgather, ffull, dense, outv,
    in_sem, s1_sem, r1_sem, s2_sem, r2_sem, fs_sem, fr_sem, o_sem,
):
    pieces, where = piece_tables()
    me = lax.axis_index("row")
    barrier = pltpu.get_barrier_semaphore()
    load = pltpu.make_async_copy(amp_hbm, amp, in_sem)
    load.start()
    for d in range(1, NR):
        pl.semaphore_signal(barrier, inc=1, device_id={"row": (me + d) % NR}, device_id_type=MESH)
    load.wait()

    @pl.loop(0, SLOTS)
    def _(slot):
        for m in range(NR):
            for j, (x, y, h) in enumerate(pieces[m]):
                send1[m, pl.ds(slot * PIECE + j, 1), :] = amp[slot, x, pl.ds(y, 1), pl.ds(h * LANES, LANES)]

    pl.semaphore_wait(barrier, NR - 1)

    def phase1(d):
        to = (me + d) % NR
        return pltpu.make_async_remote_copy(
            src_ref=send1.at[to], dst_ref=recv1.at[me, pl.ds(8, SROWS)], send_sem=s1_sem.at[to], recv_sem=r1_sem.at[me],
            device_id={"row": to}, device_id_type=MESH)

    def fock_copy(d):
        to = (me + d) % NR
        return pltpu.make_async_remote_copy(
            src_ref=fock_ref, dst_ref=fgather.at[me], send_sem=fs_sem.at[to], recv_sem=fr_sem.at[me],
            device_id={"row": to}, device_id_type=MESH)

    def phase2(d):
        to = (me + d) % NR
        return pltpu.make_async_remote_copy(
            src_ref=send2.at[to], dst_ref=recv2.at[me], send_sem=s2_sem.at[to], recv_sem=r2_sem.at[me],
            device_id={"row": to}, device_id_type=MESH)

    @pl.loop(1, NR)
    def _(d):
        phase1(d).start()

    @pl.loop(1, NR)
    def _(d):
        fock_copy(d).start()

    recv1[me, pl.ds(8, SROWS), :] = send1[me]
    fgather[me] = fock_ref[...]
    row = lax.broadcasted_iota(jnp.int32, (16, LANES), 0)
    is_pair = (row < 10) | ((row < 12) & (me < TYPE_A))
    odd = row % 2 == 1
    one = jnp.ones((16, LANES), jnp.float32)
    zero = jnp.zeros((16, LANES), jnp.float32)
    coef_a[0] = one
    coef_b[0] = zero
    coef_a[1] = jnp.where(is_pair, 0.0, -one)
    coef_b[1] = jnp.where(is_pair, -one, 0.0)
    coef_a[2] = jnp.where(is_pair & ~odd, one, 0.0)
    coef_b[2] = jnp.where(is_pair & odd, -one, 0.0)
    up_mask = ((row % 2 == 0) & (row < 12))[:PIECE]

    @pl.loop(1, NR)
    def _(d):
        src = (me + d) % NR
        pltpu.make_async_remote_copy(
            src_ref=send1.at[src], dst_ref=recv1.at[src, pl.ds(8, SROWS)], send_sem=s1_sem.at[src], recv_sem=r1_sem.at[src],
            device_id={"row": src}, device_id_type=MESH).wait_recv()

    def pack2(to, dst):
        for c in range(NT):
            code = table_ref[to, c]
            at = code // 4
            kind = code % 4
            s = at // SROWS
            r = at % SROWS
            v = recv1[s, pl.ds(r + 8, PIECE), :]
            swapped = jnp.where(up_mask, recv1[s, pl.ds(r + 9, PIECE), :], recv1[s, pl.ds(r + 7, PIECE), :])
            dst[to if dst is send2 else me, pl.ds(c * PIECE, PIECE), :] = (
                coef_a[kind, :PIECE] * v + coef_b[kind, :PIECE] * swapped)

    @pl.loop(1, NR)
    def _(d):
        pack2((me + d) % NR, send2)
        phase2(d).start()

    pack2(me, recv2)

    @pl.loop(1, NR)
    def _(d):
        src = (me + d) % NR
        pltpu.make_async_remote_copy(
            src_ref=fock_ref, dst_ref=fgather.at[src], send_sem=fs_sem.at[src], recv_sem=fr_sem.at[src],
            device_id={"row": src}, device_id_type=MESH).wait_recv()

    for d in range(NR):
        ffull[pl.ds(d * BT, BT), :] = fgather[d]

    @pl.loop(1, NR)
    def _(d):
        src = (me + d) % NR
        pltpu.make_async_remote_copy(
            src_ref=send2.at[src], dst_ref=recv2.at[src], send_sem=s2_sem.at[src], recv_sem=r2_sem.at[src],
            device_id={"row": src}, device_id_type=MESH).wait_recv()

    f = ffull[...]
    for y in range(BT):
        for h in range(2):
            for x in range(BT):
                m, j = where[(x, y, h)]
                dense[h, y, pl.ds(x, NT, stride=BT), :] = recv2[m, pl.ds(j, NT, stride=PIECE), :]
    for y in range(BT):
        column = jnp.concatenate([dense[0, y], dense[1, y]], axis=1)
        outv[y] = jnp.dot(f, column, precision=lax.Precision.HIGHEST, preferred_element_type=jnp.float32)
        pltpu.make_async_copy(outv.at[y], out_hbm.at[0, y], o_sem.at[y]).start()

    @pl.loop(1, NR)
    def _(d):
        phase1(d).wait_send()
        fock_copy(d).wait_send()
        phase2(d).wait_send()

    for y in range(BT):
        pltpu.make_async_copy(outv.at[y], out_hbm.at[0, y], o_sem.at[y]).wait()


def body(amplitudes, old_blocks, old_counts, new_phase, fock):
    e = lax.broadcasted_iota(jnp.int32, (NR, NT, NR * SLOTS), 0)
    c = lax.broadcasted_iota(jnp.int32, (NR, NT, NR * SLOTS), 1)
    live = (jnp.arange(SLOTS, dtype=jnp.int32)[None, :] < old_counts[:, None])
    ids = jnp.where(live, old_blocks, -1).reshape(1, 1, -1)
    b = (e - new_phase[0] + NR) % NR
    low = jnp.minimum(b, c)
    high = jnp.maximum(b, c)
    ident = low * NT - low * (low - 1) // 2 + (high - low)
    where_at = np.arange(NR)[:, None] * SROWS + np.arange(SLOTS)[None, :] * PIECE
    at = jnp.sum(jnp.where(ids == ident, jnp.asarray(where_at.reshape(1, 1, -1), jnp.int32), 0), axis=2)
    b2 = b[:, :, 0]
    c2 = c[:, :, 0]
    kind = jnp.where(c2 < b2, 0, jnp.where(c2 > b2, 1, 2))
    table = at * 4 + kind
    nocc = amplitudes.shape[3]
    return pl.pallas_call(
        kernel,
        name="fock_two_phase",
        out_shape=jax.ShapeDtypeStruct((1, BT, NT * BT, nocc), jnp.float32),
        in_specs=[
            pl.BlockSpec(memory_space=pltpu.SMEM),
            pl.BlockSpec(memory_space=pl.ANY),
            pl.BlockSpec(memory_space=pltpu.VMEM),
        ],
        out_specs=pl.BlockSpec(memory_space=pl.ANY),
        scratch_shapes=[
            pltpu.VMEM(amplitudes.shape, jnp.float32),
            pltpu.VMEM((NR, SROWS, LANES), jnp.float32),
            pltpu.VMEM((NR, 8 + SROWS + 8, LANES), jnp.float32),
            pltpu.VMEM((NR, CROWS, LANES), jnp.float32),
            pltpu.VMEM((NR, CROWS, LANES), jnp.float32),
            pltpu.VMEM((3, 16, LANES), jnp.float32),
            pltpu.VMEM((3, 16, LANES), jnp.float32),
            pltpu.VMEM((NR, BT, NT * BT), jnp.float32),
            pltpu.VMEM((NT * BT, NT * BT), jnp.float32),
            pltpu.VMEM((2, BT, NT * BT, LANES), jnp.float32),
            pltpu.VMEM((BT, NT * BT, nocc), jnp.float32),
            pltpu.SemaphoreType.DMA,
            pltpu.SemaphoreType.DMA((NR,)),
            pltpu.SemaphoreType.DMA((NR,)),
            pltpu.SemaphoreType.DMA((NR,)),
            pltpu.SemaphoreType.DMA((NR,)),
            pltpu.SemaphoreType.DMA((NR,)),
            pltpu.SemaphoreType.DMA((NR,)),
            pltpu.SemaphoreType.DMA((BT,)),
        ],
        compiler_params=pltpu.CompilerParams(
            collective_id=0, has_side_effects=True, vmem_limit_bytes=48 << 20),
    )(table, amplitudes, fock)


def solution(mesh):
    return jax.shard_map(
        body,
        mesh=mesh,
        in_specs=(P("row", None, None, "col"), P(), P(), P(), P("row", None)),
        out_specs=P("row", None, None, "col"),
        check_vma=False,
    )
```

time: 155 us -> 61.6 us (0.40)
  waiting for transfers between devices: 60.9 us -> 0 us
  Pallas kernels: 0 us -> 56.4 us
  local copies, waits for them, and re-layouts: 40.9 us -> 2.02 us
  starting transfers between devices: 23.3 us -> 0 us
  matrix products: 15.3 us -> 0 us
  other arithmetic: 12.4 us -> 2.05 us
    all_to_all x4 -> x0, waiting for transfers between devices: 60.9 us -> none  [the longest x3 60.9 us: several_exchanges(): lax.all_to_all(piece, axis, split_axis=0, concat_axis=0, tiled=True)]
    pallas_call x0 -> x1, Pallas kernels: none -> 56.4 us  [body(): pl.pallas_call(kernel, name='fock_two_phase', out_shape=jax.ShapeDtypeStr...]
    all_to_all x4 -> x0, starting transfers between devices: 23.3 us -> none  [the longest x3 19.1 us: several_exchanges(): lax.all_to_all(piece, axis, split_axis=0, concat_axis=0, tiled=True)]
    dot_general x3 -> x0, matrix products: 15.3 us -> none  [the longest x1 7.54 us: body(): chosen = jnp.dot(picker, received, precision=lax.Precision.HIGHEST)]
    split x5 -> x0, local copies, waits for them, and re-layouts: 9.07 us -> none  [several_exchanges(): jnp.split(parts, piece_ends(parts.shape[split_at], pieces), axis=split_at)]
    concatenate x1 -> x0, other arithmetic: 7.12 us -> none  [several_exchanges(): return joined_along(jnp.concatenate(finished, axis=split_at), concat_dim)]
    dot_general x1 -> x0, local copies, waits for them, and re-layouts: 6.86 us -> none  [body(): chosen = jnp.dot(picker, received, precision=lax.Precision.HIGHEST)]
    another operation x1 -> x0, local copies, waits for them, and re-layouts: 5.84 us -> none  [body(): received = received.reshape(-1, tile * tile * occ_dev)]
  transfers between devices with their start and end apart: 4 -> 0, of which waited for: 3 -> 0; matrix products, arithmetic and copies ran while one was open for 14% -> 0% of each run, Pallas kernels for 0% -> 0%
where the time goes in v1:
time: 61.6 us; the launch traced here: 61.4 us
  Pallas kernels  56.4 us (92%)
  other arithmetic  2.05 us (3%)
  local copies, waits for them, and re-layouts  2.02 us (3%)
  between operations  0.84 us (1%)
    pallas_call x1, Pallas kernels, body(): pl.pallas_call(kernel, name='fock_two_phase', out_shape=jax.ShapeDtypeStr...  56.4 us
    unnamed x6, local copies, waits for them, and re-layouts  1.94 us
    select_n x1, other arithmetic, body(): b = (e - new_phase[0] + NR) % NR  1.25 us

profile of v1, /device:TPU:0, one launch (start us, length us, event | category | flops | bytes accessed | tf_op | source)
XLA Modules:
  0.0 61.4 jit_solution(7764338246425414418)
XLA Ops:
  0.0 0.0 copy-start.1
  0.8 0.8 %fusion.5 = s32[16,12]{1,0:T(8,128)S(1)} fusion(s32[16,12]{1,0:T(8,128)} %param.7, s32[16]{0:T(128)} %param.8), kind=kLoop, calls=%fused_computation.18 | loop fusion | flops 384 | bytes 1600 | tf_op jit(solution)/shard_map/jit(_where)/select_n | solution.py:170
  1.6 0.1 eq.12
  1.7 1.2 %broadcast_select_fusion = (s32[16,16,192]{1,0,2:T(8,128)S(1)}, s32[16,16]{1,0:T(8,128)S(1)}) fusion(s32[16]{0:T(128)S(1)} %get-tuple-element.7, s32[16]{0:T(128)S(1)} %get-tuple-element.8, pred[16]{0:T(512)(128)(4,1)S(1)} %compare_and_fusion, s32[192]{0:T(256)} %constant.42, s32[192]{0:T(256)S(1)} %eq.12), kind=kLoop, calls=%fused_computation.13 | loop fusion | flops 1326848 | bytes 199312 | tf_op jit(solution)/shard_map/jit(remainder)/select_n | solution.py:171
  2.9 0.0 copy-done.1
  3.0 0.0 copy-start
  3.0 0.8 %copy.7.amp_hbm = f32[12,10,10,256]{3,2,1,0:T(8,128)S(1)} copy(f32[12,10,10,256]{3,0,2,1:T(8,128)S(1)} %copy-done.1) | data formatting | bytes 2457600 | tf_op args[0]
  3.7 0.0 copy-done
  3.7 56.4 %fock_two_phase.1 = f32[1,10,160,256]{3,2,1,0:T(8,128)S(1)} custom-call(s32[16,16]{1,0:T(8,128)S(1)} %bitcast_add_fusion.table_ref, f32[12,10,10,256]{3,2,1,0:T(8,128)S(1)} %copy.7.amp_hbm, f32[10,160]{1,0:T(8,128)S(1)} %copy-done), custom_call_target="tpu_custom_call" | custom-call | tf_op jit(solution)/shard_map/fock_two_phase/pallas_call | solution.py:182
  60.2 1.2 %copy.10 = f32[1,10,160,256]{3,2,1,0:T(8,128)} copy(f32[1,10,160,256]{3,2,1,0:T(8,128)S(1)} %fock_two_phase.1) | data formatting | bytes 3276800
  (3 shorter events, 0.0 us)
Async XLA Ops:
  0.0 2.9 %copy-start.1 = (f32[12,10,10,256]{3,0,2,1:T(8,128)S(1)}, f32[12,10,10,256]{3,0,2,1:T(8,128)}, u32[]{:S(2)}) copy-start(f32[12,10,10,256]{3,0,2,1:T(8,128)} %param.6) | copy-start | bytes 3686404
  3.0 0.8 %copy-start = (f32[10,160]{1,0:T(8,128)S(1)}, f32[10,160]{1,0:T(8,128)}, u32[]{:S(2)}) copy-start(f32[10,160]{1,0:T(8,128)} %fock_ref.1) | copy-start | bytes 19204

commit v2 on v0

v2 whole, which is shorter than its diff:
```python
import jax
import jax.numpy as jnp
from jax import lax
from jax.experimental import pallas as pl
from jax.experimental.pallas import tpu as pltpu
from jax.sharding import PartitionSpec as P

NT = 16
BT = 10
NR = 16
SLOTS = 12
LANES = 128
SPLIT = 8
MESH = pl.DeviceIdType.MESH
S1 = 160
R1 = 128
FRONT = 16
P2 = 208
LATE = 128
OTHERS = NT - 1
HEAD = (SPLIT // 2, 2)
ROWS1 = SPLIT * SLOTS
ROWS2 = SPLIT * OTHERS + HEAD[0]


def is_long(m):
    return (m // 4 + m) % 2 == 0


def late_rows1(long):
    return (5 if long else 4) * SLOTS


def late_rows2(long):
    return (5 if long else 4) * OTHERS + HEAD[1]


def piece_tables():
    pairs = [(x, y, h) for h in range(2) for x in range(BT) for y in range(x + 1, BT)]
    diagonal = [(x, x, h) for h in range(2) for x in range(BT)]
    pieces = []
    for m in range(NR):
        rows = []
        for _ in range(6 if is_long(m) or m in (1, 14) else 5):
            x, y, h = pairs.pop(0)
            rows += [(x, y, h), (y, x, h)]
        while len(rows) < (13 if is_long(m) else 12):
            rows.append(diagonal.pop(0))
        pieces.append(rows)
    assert not pairs and not diagonal
    return pieces


def remote(src, dst, send, recv, to):
    return pltpu.make_async_remote_copy(
        src_ref=src, dst_ref=dst, send_sem=send, recv_sem=recv, device_id=to, device_id_type=MESH)


def wait_rows(ref, rows, sem):
    part = ref.at[pl.ds(0, rows)]
    pltpu.make_async_copy(part, part, sem).wait()


def kernel(
    phase_ref, blocks_hbm, counts_hbm, amp_hbm, fock_hbm, out_ref,
    blocks_ref, counts_ref, fock_ref, amp, send1, first1, second1, send2, recv2, coef_a, coef_b,
    ftiles, fgather, ffull, turned_high, turned_low, dense, vtable, table,
    a_sem, b_sem, c_sem, f_sem, t_sem, s1_sem, r1_sem, s2_sem, r2_sem, fs_sem, fr_sem, ds_sem, dr_sem,
):
    pieces = piece_tables()
    me = lax.axis_index("row")
    col = lax.axis_index("col")
    core = col % 2
    partner = col + 1 - 2 * core
    long = is_long(me)
    barrier = pltpu.get_barrier_semaphore()
    load = pltpu.make_async_copy(amp_hbm, amp, a_sem)
    load.start()
    small = [
        pltpu.make_async_copy(blocks_hbm, blocks_ref, b_sem),
        pltpu.make_async_copy(counts_hbm, counts_ref, c_sem),
        pltpu.make_async_copy(fock_hbm, fock_ref, f_sem),
    ]
    for copy in small:
        copy.start()
    for d in range(1, NR):
        pl.semaphore_signal(barrier, inc=1, device_id={"row": (me + d) % NR}, device_id_type=MESH)
    pl.semaphore_signal(barrier, inc=1, device_id={"col": partner}, device_id_type=MESH)
    with jax.named_scope("load"):
        load.wait()

    with jax.named_scope("pack1"):
        for m in range(NR):
            for j, (x, y, h) in enumerate(pieces[m]):
                send1[pl.ds(m * S1 + j * SLOTS, SLOTS), :] = amp[x, y, :, pl.ds(h * LANES, LANES)]

    for copy in small:
        copy.wait()
    ftiles[0] = fock_ref[:8, :LANES]
    ftiles[1, :2] = fock_ref[8:, :LANES]
    ftiles[1, 2:8, :32] = fock_ref[:6, LANES:]
    ftiles[1, 2:6, 32:64] = fock_ref[6:, LANES:]

    with jax.named_scope("barrier"):
        pl.semaphore_wait(barrier, NR)

    def early1(to):
        return remote(
            send1.at[pl.ds(to * S1, ROWS1)], first1.at[pl.ds(me * R1 + FRONT, ROWS1)],
            s1_sem, r1_sem.at[0], {"row": to})

    def late1(to, rows):
        return remote(
            send1.at[pl.ds(to * S1 + ROWS1, rows)], second1.at[pl.ds(me * R1 + FRONT, rows)],
            s1_sem, r1_sem.at[1], {"row": to})

    def early2(to):
        return remote(
            send2.at[pl.ds(to * P2, ROWS2)], recv2.at[pl.ds(me * P2, ROWS2)],
            s2_sem, r2_sem.at[0], {"row": to})

    def late2(to, rows):
        return remote(
            send2.at[pl.ds(to * P2 + LATE, rows)], recv2.at[pl.ds(me * P2 + LATE, rows)],
            s2_sem, r2_sem.at[1], {"row": to})

    def fock_copy(to):
        return remote(ftiles.at[core], fgather.at[core, me], fs_sem, fr_sem, {"row": to})

    exchange = remote(fgather.at[core], fgather.at[core], ds_sem, dr_sem, {"col": partner})

    def both(flag, action):
        for value in (True, False):
            @pl.when(flag == value)
            def _():
                action(value)

    with jax.named_scope("start1"):
        @pl.loop(1, NR)
        def _(d):
            early1((me + d) % NR).start()

        @pl.loop(1, NR)
        def _(d):
            to = (me + d) % NR
            both(is_long(to), lambda value: late1(to, late_rows1(value)).start())

        @pl.loop(1, NR)
        def _(d):
            fock_copy((me + d) % NR).start()

    with jax.named_scope("tables"):
        first1[pl.ds(me * R1 + FRONT, ROWS1), :] = send1[pl.ds(me * S1, ROWS1), :]
        second1[pl.ds(me * R1 + FRONT, S1 - ROWS1), :] = send1[pl.ds(me * S1 + ROWS1, S1 - ROWS1), :]
        fgather[core, me] = ftiles[core]
        row = lax.broadcasted_iota(jnp.int32, (16, LANES), 0)
        is_pair = (row < 10) | ((row < 12) & (long | (me == 1) | (me == 14)))
        one = jnp.ones((16, LANES), jnp.float32)
        coef_a[0] = one
        coef_b[0] = jnp.zeros((16, LANES), jnp.float32)
        coef_a[1] = jnp.where(is_pair, 0.0, -one)
        coef_b[1] = jnp.where(is_pair, -one, 0.0)
        up_mask = (row % 2 == 0) & (row < 12)

        sub = lax.broadcasted_iota(jnp.int32, (8, LANES), 0)
        lane = lax.broadcasted_iota(jnp.int32, (8, LANES), 1)
        mine = ((sub % 2) * 8 + lane // NT - phase_ref[0] + NR) % NR
        other = (mine + lane) % NT
        low = jnp.minimum(mine, other)
        high = jnp.maximum(mine, other)
        ident = low * NT - (low * (low - 1)) // 2 + (high - low)

        def look(d, at):
            for slot in range(SLOTS):
                block = jnp.where(slot < counts_ref[d], blocks_ref[d, slot], -1)
                at = jnp.where(ident == block, d * R1 + (FRONT + slot), at)
            return at

        at = lax.fori_loop(0, NR, look, jnp.full((8, LANES), FRONT, jnp.int32))
        vtable[...] = jnp.where(sub < 2, at, jnp.where(other > mine, 1, 0))
        to_smem = pltpu.make_async_copy(vtable, table, t_sem)
        to_smem.start()
        to_smem.wait()

    def pack2(k, to, dst, slot):
        first = SPLIT * k
        n = SPLIT if k == 0 else 5
        base = slot * P2 + LATE * k
        recv1 = (first1, second1)[k]
        for c in range(NT):
            at = table[to // 8, (to % 8) * NT + c]
            if c == 0:
                dst[pl.ds(base, HEAD[k]), :] = recv1[pl.ds(at, HEAD[k], stride=2 * SLOTS), :]
                continue
            kind = table[2 + to // 8, (to % 8) * NT + c]
            v = recv1[pl.ds(at, n, stride=SLOTS), :]
            up = recv1[pl.ds(at + SLOTS, n, stride=SLOTS), :]
            down = recv1[pl.ds(at - SLOTS, n, stride=SLOTS), :]
            swapped = jnp.where(up_mask[first:first + n], up, down)
            dst[pl.ds(base + HEAD[k] + c - 1, n, stride=OTHERS), :] = (
                coef_a[kind, first:first + n] * v + coef_b[kind, first:first + n] * swapped)

    with jax.named_scope("wait1_0"):
        wait_rows(first1, OTHERS * ROWS1, r1_sem.at[0])

    with jax.named_scope("pack2_0"):
        @pl.loop(1, NR)
        def _(d):
            to = (me + d) % NR
            pack2(0, to, send2, to)
            early2(to).start()

        pack2(0, me, recv2, me)

    with jax.named_scope("wait1_1"):
        both(long, lambda value: wait_rows(second1, OTHERS * late_rows1(value), r1_sem.at[1]))

    with jax.named_scope("pack2_1"):
        @pl.loop(1, NR)
        def _(d):
            to = (me + d) % NR
            pack2(1, to, send2, to)
            both(long, lambda value: late2(to, late_rows2(value)).start())

        pack2(1, me, recv2, me)

    with jax.named_scope("waitf"):
        wait_rows(send1, OTHERS * 8, fr_sem)
        exchange.start()
        both(long, lambda value: wait_rows(
            send1, OTHERS * ROWS1 + (8 - value) * late_rows1(True) + (7 + value) * late_rows1(False), s1_sem))

    def assemble(first, last):
        for m in range(NR):
            for j, (x, y, h) in enumerate(pieces[m]):
                if not first <= j < last:
                    continue
                k = int(j >= SPLIT)
                base = m * P2 + LATE * k
                rows = recv2[pl.ds(base + HEAD[k] + (j - SPLIT * k) * OTHERS, OTHERS), :]
                dense[h, y, pl.ds(x + BT, OTHERS, stride=BT), :] = rows
                if x < y:
                    head = recv2[pl.ds(base + (j - SPLIT * k) // 2, 1), :]
                    dense[h, y, pl.ds(x, 1), :] = head
                    dense[h, x, pl.ds(y, 1), :] = -head
                elif x == y:
                    dense[h, y, pl.ds(x, 1), :] = jnp.zeros((1, LANES), jnp.float32)

    with jax.named_scope("wait2_0"):
        wait_rows(recv2, OTHERS * ROWS2, r2_sem.at[0])

    with jax.named_scope("assemble_0"):
        assemble(0, SPLIT)

    with jax.named_scope("fock"):
        exchange.wait()
        wait_rows(send1, OTHERS * 8, fs_sem)
        for d in range(NR):
            at = d * BT
            ffull[pl.ds(at, 8), :LANES] = fgather[0, d]
            ffull[pl.ds(at + 8, 2), :LANES] = fgather[1, d, :2]
            ffull[pl.ds(at, 6), LANES:] = fgather[1, d, 2:8, :32]
            ffull[pl.ds(at + 6, 4), LANES:] = fgather[1, d, 2:6, 32:64]
        turn = (me - phase_ref[0] + NR) % NR * BT
        size = NT * BT
        shifted = lax.broadcasted_iota(jnp.int32, (size, size), 1) + turn
        shifted = jnp.where(shifted >= size, shifted - size, shifted)
        picks = (lax.broadcasted_iota(jnp.int32, (size, size), 0) == shifted).astype(jnp.float32).astype(jnp.bfloat16)
        f = ffull[...]
        f_high = f.astype(jnp.bfloat16)
        f_low = (f - f_high.astype(jnp.float32)).astype(jnp.bfloat16)
        turned_high[...] = jnp.dot(f_high, picks, preferred_element_type=jnp.float32).astype(jnp.bfloat16)
        turned_low[...] = jnp.dot(f_low, picks, preferred_element_type=jnp.float32).astype(jnp.bfloat16)

    with jax.named_scope("wait2_1"):
        both(long, lambda value: wait_rows(
            recv2, (8 - value) * late_rows2(True) + (7 + value) * late_rows2(False), r2_sem.at[1]))

    with jax.named_scope("assemble_1"):
        assemble(SPLIT, 13)

    with jax.named_scope("matmul"):
        f_high = turned_high[...]
        f_low = turned_low[...]
        for y in range(BT):
            column = jnp.concatenate([dense[0, y], dense[1, y]], axis=1)
            c_high = column.astype(jnp.bfloat16)
            c_low = (column - c_high.astype(jnp.float32)).astype(jnp.bfloat16)
            out_ref[0, y] = (
                jnp.dot(f_high, c_high, preferred_element_type=jnp.float32)
                + jnp.dot(f_high, c_low, preferred_element_type=jnp.float32)
                + jnp.dot(f_low, c_high, preferred_element_type=jnp.float32))

    with jax.named_scope("drain"):
        both(long, lambda value: wait_rows(send2, OTHERS * (ROWS2 + late_rows2(value)), s2_sem))


def body(amplitudes, old_blocks, old_counts, new_phase, fock):
    nocc = amplitudes.shape[3]
    turned = jnp.transpose(amplitudes, (1, 2, 0, 3))
    hbm = pl.BlockSpec(memory_space=pltpu.HBM)
    operands = [
        pltpu.with_memory_space_constraint(array, pltpu.HBM)
        for array in (old_blocks, old_counts, turned, fock)
    ]
    size = NT * BT
    return pl.pallas_call(
        kernel,
        name="fock_two_phase",
        out_shape=jax.ShapeDtypeStruct((1, BT, size, nocc), jnp.float32),
        in_specs=[pl.BlockSpec(memory_space=pltpu.SMEM)] + [hbm] * 4,
        out_specs=pl.BlockSpec(memory_space=pltpu.VMEM),
        scratch_shapes=[
            pltpu.SMEM(old_blocks.shape, jnp.int32),
            pltpu.SMEM(old_counts.shape, jnp.int32),
            pltpu.VMEM(fock.shape, jnp.float32),
            pltpu.VMEM(turned.shape, jnp.float32),
            pltpu.VMEM((NR * S1, LANES), jnp.float32),
            pltpu.VMEM((NR * R1, LANES), jnp.float32),
            pltpu.VMEM((NR * R1, LANES), jnp.float32),
            pltpu.VMEM((NR * P2, LANES), jnp.float32),
            pltpu.VMEM((NR * P2, LANES), jnp.float32),
            pltpu.VMEM((2, 16, LANES), jnp.float32),
            pltpu.VMEM((2, 16, LANES), jnp.float32),
            pltpu.VMEM((2, 8, LANES), jnp.float32),
            pltpu.VMEM((2, NR, 8, LANES), jnp.float32),
            pltpu.VMEM((size, size), jnp.float32),
            pltpu.VMEM((size, size), jnp.bfloat16),
            pltpu.VMEM((size, size), jnp.bfloat16),
            pltpu.VMEM((2, BT, size, LANES), jnp.float32),
            pltpu.VMEM((8, LANES), jnp.int32),
            pltpu.SMEM((8, LANES), jnp.int32),
        ] + [pltpu.SemaphoreType.DMA] * 6 + [
            pltpu.SemaphoreType.DMA((2,)),
            pltpu.SemaphoreType.DMA,
            pltpu.SemaphoreType.DMA((2,)),
        ] + [pltpu.SemaphoreType.DMA] * 4,
        compiler_params=pltpu.CompilerParams(
            collective_id=0, has_side_effects=True, vmem_limit_bytes=48 << 20),
    )(new_phase, *operands)


def solution(mesh):
    return jax.shard_map(
        body,
        mesh=mesh,
        in_specs=(P("row", None, None, "col"), P(), P(), P(), P("row", None)),
        out_specs=P("row", None, None, "col"),
        check_vma=False,
    )
```

time: 155 us -> 42.9 us (0.28)
  waiting for transfers between devices: 60.9 us -> 0 us
  Pallas kernels: 0 us -> 40.8 us
  local copies, waits for them, and re-layouts: 40.9 us -> 1.17 us
  starting transfers between devices: 23.3 us -> 0 us
  matrix products: 15.3 us -> 0 us
  other arithmetic: 12.4 us -> 0 us
    all_to_all x4 -> x0, waiting for transfers between devices: 60.9 us -> none  [the longest x3 60.9 us: several_exchanges(): lax.all_to_all(piece, axis, split_axis=0, concat_axis=0, tiled=True)]
    pallas_call x0 -> x1, Pallas kernels: none -> 40.8 us  [body(): pl.pallas_call(kernel, name='fock_two_phase', out_shape=jax.ShapeDtypeStr...]
    all_to_all x4 -> x0, starting transfers between devices: 23.3 us -> none  [the longest x3 19.1 us: several_exchanges(): lax.all_to_all(piece, axis, split_axis=0, concat_axis=0, tiled=True)]
    dot_general x3 -> x0, matrix products: 15.3 us -> none  [the longest x1 7.54 us: body(): chosen = jnp.dot(picker, received, precision=lax.Precision.HIGHEST)]
    split x5 -> x0, local copies, waits for them, and re-layouts: 9.07 us -> none  [several_exchanges(): jnp.split(parts, piece_ends(parts.shape[split_at], pieces), axis=split_at)]
    concatenate x1 -> x0, other arithmetic: 7.12 us -> none  [several_exchanges(): return joined_along(jnp.concatenate(finished, axis=split_at), concat_dim)]
    dot_general x1 -> x0, local copies, waits for them, and re-layouts: 6.86 us -> none  [body(): chosen = jnp.dot(picker, received, precision=lax.Precision.HIGHEST)]
    unnamed x15 -> x1, local copies, waits for them, and re-layouts: 7.43 us -> 1.17 us
  transfers between devices with their start and end apart: 4 -> 0, of which waited for: 3 -> 0; matrix products, arithmetic and copies ran while one was open for 14% -> 0% of each run, Pallas kernels for 0% -> 0%
where the time goes in v2:
time: 42.9 us; the launch traced here: 42.7 us
  Pallas kernels  40.8 us (95%)
  local copies, waits for them, and re-layouts  1.17 us (3%)
  between operations  0.66 us (2%)
    pallas_call x1, Pallas kernels, body(): pl.pallas_call(kernel, name='fock_two_phase', out_shape=jax.ShapeDtypeStr...  40.8 us
    unnamed x1, local copies, waits for them, and re-layouts  1.17 us

profile of v2, /device:TPU:0, one launch (start us, length us, event | category | flops | bytes accessed | tf_op | source)
XLA Modules:
  0.0 42.7 jit_solution(12110866632922591182)
XLA Ops:
  0.7 40.8 %fock_two_phase.1 = f32[1,10,160,256]{3,2,1,0:T(8,128)S(1)} custom-call(s32[1]{0:T(128)S(6)} %copy.7.phase_ref, s32[16,12]{1,0:T(8,128)} %blocks_hbm.1, s32[16]{0:T(128)} %counts_hbm.1, f32[10,10,12,256]{3,2,1,0:T(8,128)} %bitcast.1, f32[10,160]{1,0:T(8,128)} %fock_hbm.1), custom_call_target="tpu_custom_call" | custom-call | tf_op jit(solution)/shard_map/fock_two_phase/pallas_call | solution.py:307
  41.5 1.2 %copy.8 = f32[1,10,160,256]{3,2,1,0:T(8,128)} copy(f32[1,10,160,256]{3,2,1,0:T(8,128)S(1)} %fock_two_phase.1) | data formatting | bytes 3276800

commit v3 on v2

--- a/solution.py
+++ b/solution.py
@@ -11,6 +11,9 @@
 SLOTS = 12
 LANES = 128
 SPLIT = 8
+EARLY = 4
+TWO_EARLY = (1, 4, 11, 14)
+TWO_LATE = (3, 12)
 MESH = pl.DeviceIdType.MESH
 S1 = 160
 R1 = 128
@@ -36,18 +39,24 @@
 
 
 def piece_tables():
-    pairs = [(x, y, h) for h in range(2) for x in range(BT) for y in range(x + 1, BT)]
-    diagonal = [(x, x, h) for h in range(2) for x in range(BT)]
+    halves = range(2)
+    pairs = [[], []]
+    diagonal = [[], []]
+    for h in halves:
+        for x in range(BT):
+            diagonal[x >= EARLY].append((x, x, h))
+            pairs[x >= EARLY] += [(x, y, h) for y in range(x + 1, BT)]
     pieces = []
     for m in range(NR):
         rows = []
-        for _ in range(6 if is_long(m) or m in (1, 14) else 5):
-            x, y, h = pairs.pop(0)
-            rows += [(x, y, h), (y, x, h)]
-        while len(rows) < (13 if is_long(m) else 12):
-            rows.append(diagonal.pop(0))
+        for k, count, size in ((0, 3 if m in TWO_EARLY else 4, SPLIT), (1, 1 if m in TWO_LATE else 2, 13 if is_long(m) else 12)):
+            for _ in range(count):
+                x, y, h = pairs[k].pop(0)
+                rows += [(x, y, h), (y, x, h)]
+            while len(rows) < size:
+                rows.append(diagonal[k].pop(0))
         pieces.append(rows)
-    assert not pairs and not diagonal
+    assert not any(pairs) and not any(diagonal)
     return pieces
 
 
@@ -61,10 +70,23 @@
     pltpu.make_async_copy(part, part, sem).wait()
 
 
+def contract(high_ref, low_ref, dense, columns, out):
+    f_high = high_ref[...]
+    f_low = low_ref[...]
+    for y in columns:
+        column = jnp.concatenate([dense[0, y], dense[1, y]], axis=1)
+        c_high = column.astype(jnp.bfloat16)
+        c_low = (column - c_high.astype(jnp.float32)).astype(jnp.bfloat16)
+        out[y] = (
+            jnp.dot(f_high, c_high, preferred_element_type=jnp.float32)
+            + jnp.dot(f_high, c_low, preferred_element_type=jnp.float32)
+            + jnp.dot(f_low, c_high, preferred_element_type=jnp.float32))
+
+
 def kernel(
-    phase_ref, blocks_hbm, counts_hbm, amp_hbm, fock_hbm, out_ref,
+    phase_ref, blocks_hbm, counts_hbm, amp_hbm, fock_hbm, head_ref, dense, high_ref, low_ref,
     blocks_ref, counts_ref, fock_ref, amp, send1, first1, second1, send2, recv2, coef_a, coef_b,
-    ftiles, fgather, ffull, turned_high, turned_low, dense, vtable, table,
+    ftiles, fgather, ffull, early, vtable, table,
     a_sem, b_sem, c_sem, f_sem, t_sem, s1_sem, r1_sem, s2_sem, r2_sem, fs_sem, fr_sem, ds_sem, dr_sem,
 ):
     pieces = piece_tables()
@@ -154,7 +176,9 @@
         second1[pl.ds(me * R1 + FRONT, S1 - ROWS1), :] = send1[pl.ds(me * S1 + ROWS1, S1 - ROWS1), :]
         fgather[core, me] = ftiles[core]
         row = lax.broadcasted_iota(jnp.int32, (16, LANES), 0)
-        is_pair = (row < 10) | ((row < 12) & (long | (me == 1) | (me == 14)))
+        two_early = (me == 1) | (me == 4) | (me == 11) | (me == 14)
+        two_late = (me == 3) | (me == 12)
+        is_pair = (row < 12) & ~((row // 2 == 3) & two_early) & ~((row // 2 == 5) & two_late)
         one = jnp.ones((16, LANES), jnp.float32)
         coef_a[0] = one
         coef_b[0] = jnp.zeros((16, LANES), jnp.float32)
@@ -230,6 +254,10 @@
         both(long, lambda value: wait_rows(
             send1, OTHERS * ROWS1 + (8 - value) * late_rows1(True) + (7 + value) * late_rows1(False), s1_sem))
 
+    def put(h, y, at, rows):
+        target, column = (early, y) if y < EARLY else (dense, y - EARLY)
+        target[h, column, at, :] = rows
+
     def assemble(first, last):
         for m in range(NR):
             for j, (x, y, h) in enumerate(pieces[m]):
@@ -238,13 +266,13 @@
                 k = int(j >= SPLIT)
                 base = m * P2 + LATE * k
                 rows = recv2[pl.ds(base + HEAD[k] + (j - SPLIT * k) * OTHERS, OTHERS), :]
-                dense[h, y, pl.ds(x + BT, OTHERS, stride=BT), :] = rows
+                put(h, y, pl.ds(x + BT, OTHERS, stride=BT), rows)
                 if x < y:
                     head = recv2[pl.ds(base + (j - SPLIT * k) // 2, 1), :]
-                    dense[h, y, pl.ds(x, 1), :] = head
-                    dense[h, x, pl.ds(y, 1), :] = -head
+                    put(h, y, pl.ds(x, 1), head)
+                    put(h, x, pl.ds(y, 1), -head)
                 elif x == y:
-                    dense[h, y, pl.ds(x, 1), :] = jnp.zeros((1, LANES), jnp.float32)
+                    put(h, y, pl.ds(x, 1), jnp.zeros((1, LANES), jnp.float32))
 
     with jax.named_scope("wait2_0"):
         wait_rows(recv2, OTHERS * ROWS2, r2_sem.at[0])
@@ -269,8 +297,11 @@
         f = ffull[...]
         f_high = f.astype(jnp.bfloat16)
         f_low = (f - f_high.astype(jnp.float32)).astype(jnp.bfloat16)
-        turned_high[...] = jnp.dot(f_high, picks, preferred_element_type=jnp.float32).astype(jnp.bfloat16)
-        turned_low[...] = jnp.dot(f_low, picks, preferred_element_type=jnp.float32).astype(jnp.bfloat16)
+        high_ref[...] = jnp.dot(f_high, picks, preferred_element_type=jnp.float32).astype(jnp.bfloat16)
+        low_ref[...] = jnp.dot(f_low, picks, preferred_element_type=jnp.float32).astype(jnp.bfloat16)
+
+    with jax.named_scope("matmul_0"):
+        contract(high_ref, low_ref, early, range(EARLY), head_ref)
 
     with jax.named_scope("wait2_1"):
         both(long, lambda value: wait_rows(
@@ -279,20 +310,19 @@
     with jax.named_scope("assemble_1"):
         assemble(SPLIT, 13)
 
-    with jax.named_scope("matmul"):
-        f_high = turned_high[...]
-        f_low = turned_low[...]
-        for y in range(BT):
-            column = jnp.concatenate([dense[0, y], dense[1, y]], axis=1)
-            c_high = column.astype(jnp.bfloat16)
-            c_low = (column - c_high.astype(jnp.float32)).astype(jnp.bfloat16)
-            out_ref[0, y] = (
-                jnp.dot(f_high, c_high, preferred_element_type=jnp.float32)
-                + jnp.dot(f_high, c_low, preferred_element_type=jnp.float32)
-                + jnp.dot(f_low, c_high, preferred_element_type=jnp.float32))
-
     with jax.named_scope("drain"):
         both(long, lambda value: wait_rows(send2, OTHERS * (ROWS2 + late_rows2(value)), s2_sem))
+
+
+def finish(head_ref, dense, high_ref, low_ref, out_hbm, late, h_sem, o_sem):
+    copies = [pltpu.make_async_copy(head_ref, out_hbm.at[0, pl.ds(0, EARLY)], h_sem)]
+    copies[0].start()
+    for y in range(BT - EARLY):
+        contract(high_ref, low_ref, dense, (y,), late)
+        copies.append(pltpu.make_async_copy(late.at[y], out_hbm.at[0, EARLY + y], o_sem.at[y]))
+        copies[-1].start()
+    for copy in copies:
+        copy.wait()
 
 
 def body(amplitudes, old_blocks, old_counts, new_phase, fock):
@@ -304,12 +334,18 @@
         for array in (old_blocks, old_counts, turned, fock)
     ]
     size = NT * BT
-    return pl.pallas_call(
+    vmem = pl.BlockSpec(memory_space=pltpu.VMEM)
+    parts = pl.pallas_call(
         kernel,
         name="fock_two_phase",
-        out_shape=jax.ShapeDtypeStruct((1, BT, size, nocc), jnp.float32),
+        out_shape=(
+            jax.ShapeDtypeStruct((EARLY, size, nocc), jnp.float32),
+            jax.ShapeDtypeStruct((2, BT - EARLY, size, LANES), jnp.float32),
+            jax.ShapeDtypeStruct((size, size), jnp.bfloat16),
+            jax.ShapeDtypeStruct((size, size), jnp.bfloat16),
+        ),
         in_specs=[pl.BlockSpec(memory_space=pltpu.SMEM)] + [hbm] * 4,
-        out_specs=pl.BlockSpec(memory_space=pltpu.VMEM),
+        out_specs=(vmem,) * 4,
         scratch_shapes=[
             pltpu.SMEM(old_blocks.shape, jnp.int32),
             pltpu.SMEM(old_counts.shape, jnp.int32),
@@ -325,9 +361,7 @@
             pltpu.VMEM((2, 8, LANES), jnp.float32),
             pltpu.VMEM((2, NR, 8, LANES), jnp.float32),
             pltpu.VMEM((size, size), jnp.float32),
-            pltpu.VMEM((size, size), jnp.bfloat16),
-            pltpu.VMEM((size, size), jnp.bfloat16),
-            pltpu.VMEM((2, BT, size, LANES), jnp.float32),
+            pltpu.VMEM((2, EARLY, size, LANES), jnp.float32),
             pltpu.VMEM((8, LANES), jnp.int32),
             pltpu.SMEM((8, LANES), jnp.int32),
         ] + [pltpu.SemaphoreType.DMA] * 6 + [
@@ -338,6 +372,19 @@
         compiler_params=pltpu.CompilerParams(
             collective_id=0, has_side_effects=True, vmem_limit_bytes=48 << 20),
     )(new_phase, *operands)
+    return pl.pallas_call(
+        finish,
+        name="fock_finish",
+        out_shape=jax.ShapeDtypeStruct((1, BT, size, nocc), jnp.float32),
+        in_specs=[vmem] * 4,
+        out_specs=hbm,
+        scratch_shapes=[
+            pltpu.VMEM((BT - EARLY, size, nocc), jnp.float32),
+            pltpu.SemaphoreType.DMA,
+            pltpu.SemaphoreType.DMA((BT - EARLY,)),
+        ],
+        compiler_params=pltpu.CompilerParams(vmem_limit_bytes=16 << 20),
+    )(*parts)
 
 
 def solution(mesh):

time: 42.9 us -> 42.3 us (0.986)
  local copies, waits for them, and re-layouts: 1.17 us -> 0 us
  Pallas kernels: 40.8 us -> 41.4 us
    unnamed x1 -> x0, local copies, waits for them, and re-layouts: 1.17 us -> none
    pallas_call x1 -> x2, Pallas kernels: 40.8 us -> 41.4 us  [the longest x1 40.1 us: body(): pl.pallas_call(kernel, name='fock_two_phase', out_shape=(jax.ShapeDtypeSt...]
where the time goes in v3:
time: 42.3 us; the launch traced here: 42.1 us
  Pallas kernels  41.4 us (98%)
  between operations  0.66 us (2%)
    pallas_call x1, Pallas kernels, body(): pl.pallas_call(kernel, name='fock_two_phase', out_shape=(jax.ShapeDtypeSt...  40.1 us
    pallas_call x1, Pallas kernels, body(): pl.pallas_call(finish, name='fock_finish', out_shape=jax.ShapeDtypeStruct...  1.33 us

profile of v3, /device:TPU:0, one launch (start us, length us, event | category | flops | bytes accessed | tf_op | source)
XLA Modules:
  0.0 42.1 jit_solution(1627550032880387836)
XLA Ops:
  0.7 40.1 %fock_two_phase.1 = (f32[4,160,256]{2,1,0:T(8,128)S(1)}, f32[2,6,160,128]{3,2,1,0:T(8,128)S(1)}, bf16[160,160]{1,0:T(8,128)(2,1)S(1)}, bf16[160,160]{1,0:T(8,128)(2,1)S(1)}) custom-call(s32[1]{0:T(128)S(6)} %copy.6.phase_ref, s32[16,12]{1,0:T(8,128)} %blocks_hbm.1, s32[16]{0:T(128)} %counts_hbm.1, f32[10,10,12,256]{3,2,1,0:T(8,128)} %bitcast.1, ...), custom_call_target="tpu_custom_call" | custom-call | tf_op jit(solution)/shard_map/fock_two_phase/pallas_call | solution.py:338
  40.7 1.3 %fock_finish.1 = f32[1,10,160,256]{3,2,1,0:T(8,128)} custom-call(f32[4,160,256]{2,1,0:T(8,128)S(1)} %get-tuple-element.9.head_ref, f32[2,6,160,128]{3,2,1,0:T(8,128)S(1)} %get-tuple-element.10.dense, bf16[160,160]{1,0:T(8,128)(2,1)S(1)} %get-tuple-element.11.high_ref, bf16[160,160]{1,0:T(8,128)(2,1)S(1)} %get-tuple-element.12.low_ref), custom_call_target="tpu_custom_call" | custom-call | tf_op jit(solution)/shard_map/fock_finish/pallas_call | solution.py:375

commit v4 on v3

v4 whole, which is shorter than its diff:
```python
import jax
import jax.numpy as jnp
from jax import lax
from jax.experimental import pallas as pl
from jax.experimental.pallas import tpu as pltpu
from jax.sharding import PartitionSpec as P

NT = 16
BT = 10
NR = 16
NC = 8
SLOTS = 12
LANES = 128
SPLIT = 8
EARLY = 4
TWO_EARLY = (1, 4, 11, 14)
TWO_LATE = (3, 12)
MESH = pl.DeviceIdType.MESH
S1 = 160
R1 = 96
FRONT = 16
OTHERS = NT - 1
CUTS = (0, 4, 8, 13)
LAST = len(CUTS) - 2
MESH = pl.DeviceIdType.MESH
S1 = 160
R1 = 96
FRONT = 16
LATE = 128
OTHERS = NT - 1
HEAD = (SPLIT // 2, 2)
ROWS1 = SPLIT * SLOTS
ROWS2 = SPLIT * OTHERS + HEAD[0]


def is_long(m):
    return (m // 4 + m) % 2 == 0


def rows_in(k, long):
    return CUTS[k + 1] - CUTS[k] - int(k == LAST and not long)


def heads_in(k):
    return (CUTS[k + 1] - CUTS[k]) // 2


def rows1(k, long):
    return rows_in(k, long) * SLOTS


def rows2(k, long):
    return rows_in(k, long) * OTHERS + heads_in(k)


def base2(k):
    return sum(-(-rows2(i, True) // 8) * 8 for i in range(k))


P2 = base2(LAST + 1)


def piece_tables():
    halves = range(2)
    pairs = [[], []]
    diagonal = [[], []]
    for h in halves:
        for x in range(BT):
            diagonal[x >= EARLY].append((x, x, h))
            pairs[x >= EARLY] += [(x, y, h) for y in range(x + 1, BT)]
    pieces = []
    for m in range(NR):
        rows = []
        for k, count, size in ((0, 3 if m in TWO_EARLY else 4, SPLIT), (1, 1 if m in TWO_LATE else 2, 13 if is_long(m) else 12)):
            for _ in range(count):
                x, y, h = pairs[k].pop(0)
                rows += [(x, y, h), (y, x, h)]
            while len(rows) < size:
                rows.append(diagonal[k].pop(0))
        pieces.append(rows)
    assert not any(pairs) and not any(diagonal)
    return pieces


def remote(src, dst, send, recv, to):
    return pltpu.make_async_remote_copy(
        src_ref=src, dst_ref=dst, send_sem=send, recv_sem=recv, device_id=to, device_id_type=MESH)


def wait_rows(ref, rows, sem):
    part = ref.at[pl.ds(0, rows)]
    pltpu.make_async_copy(part, part, sem).wait()


def contract(high_ref, low_ref, dense, columns, out):
    f_high = high_ref[...]
    f_low = low_ref[...]
    for y in columns:
        column = jnp.concatenate([dense[0, y], dense[1, y]], axis=1)
        c_high = column.astype(jnp.bfloat16)
        c_low = (column - c_high.astype(jnp.float32)).astype(jnp.bfloat16)
        out[y] = (
            jnp.dot(f_high, c_high, preferred_element_type=jnp.float32)
            + jnp.dot(f_high, c_low, preferred_element_type=jnp.float32)
            + jnp.dot(f_low, c_high, preferred_element_type=jnp.float32))


def kernel(
    phase_hbm, blocks_hbm, counts_hbm, amp_hbm, fock_hbm, head_ref, dense, high_ref, low_ref,
    phase_ref, blocks_ref, counts_ref, fock_ref, amp, send1, land0, land1, land2, send2, recv2, coef_a, coef_b,
    ftiles, fgather, ffull, early, vtable, table,
    a_sem, p_sem, b_sem, c_sem, f_sem, t_sem, s1_sem, r1_sem, s2_sem, r2_sem, fs_sem, fr_sem, ds_sem, dr_sem,
):
    pieces = piece_tables()
    me = lax.axis_index("row")
    col = lax.axis_index("col")
    long = is_long(me)
    barrier = pltpu.get_barrier_semaphore()
    loads = [
        pltpu.make_async_copy(amp_hbm.at[part], amp.at[part], a_sem.at[i])
        for i, part in enumerate((
            (pl.ds(0, EARLY),),
            (pl.ds(EARLY, BT - EARLY), pl.ds(0, EARLY)),
            (pl.ds(EARLY, BT - EARLY), pl.ds(EARLY, BT - EARLY))))
    ]
    for copy in loads:
        copy.start()
    small = [
        pltpu.make_async_copy(phase_hbm, phase_ref, p_sem),
        pltpu.make_async_copy(blocks_hbm, blocks_ref, b_sem),
        pltpu.make_async_copy(counts_hbm, counts_ref, c_sem),
        pltpu.make_async_copy(fock_hbm, fock_ref, f_sem),
    ]
    for copy in small:
        copy.start()
    for d in range(1, NR):
        pl.semaphore_signal(barrier, inc=1, device_id={"row": (me + d) % NR}, device_id_type=MESH)
    for d in range(1, NC):
        pl.semaphore_signal(barrier, inc=1, device_id={"col": (col + d) % NC}, device_id_type=MESH)
    def pack1(first, last):
        for m in range(NR):
            for j, (x, y, h) in enumerate(pieces[m]):
                if first <= j < last:
                    send1[pl.ds(m * S1 + j * SLOTS, SLOTS), :] = amp[x, y, :, pl.ds(h * LANES, LANES)]

    with jax.named_scope("load"):
        loads[0].wait()
        loads[1].wait()
    with jax.named_scope("pack1_0"):
        pack1(0, SPLIT)
    with jax.named_scope("barrier"):
        pl.semaphore_wait(barrier, NR + NC - 2)

    lands = (land0, land1, land2)

    def send_1(k, to, rows):
        return remote(
            send1.at[pl.ds(to * S1 + CUTS[k] * SLOTS, rows)], lands[k].at[pl.ds(me * R1 + FRONT, rows)],
            s1_sem, r1_sem.at[k], {"row": to})

    def send_2(k, to, rows):
        at = base2(k)
        return remote(
            send2.at[pl.ds(to * P2 + at, rows)], recv2.at[pl.ds(me * P2 + at, rows)],
            s2_sem, r2_sem.at[k], {"row": to})

    def at_size(k, flag, action):
        if k == LAST:
            both(flag, action)
        else:
            action(True)

    def fock_copy(to):
        return remote(ftiles.at[col], fgather.at[col, me], fs_sem, fr_sem, {"row": to})

    def exchange(d):
        return remote(fgather.at[col], fgather.at[col], ds_sem, dr_sem, {"col": (col + d) % NC})

    def both(flag, action):
        for value in (True, False):
            @pl.when(flag == value)
            def _():
                action(value)

    def start1(k):
        @pl.loop(1, NR)
        def _(d):
            to = (me + d) % NR
            at_size(k, is_long(to), lambda value: send_1(k, to, rows1(k, value)).start())

    with jax.named_scope("start1"):
        for k in range(LAST):
            start1(k)

    with jax.named_scope("pack1_1"):
        loads[2].wait()
        pack1(SPLIT, 13)

    with jax.named_scope("start1b"):
        start1(LAST)

    for copy in small:
        copy.wait()
    for q in range(5):
        ftiles[q] = fock_ref[2 * q:2 * q + 2, :LANES]
    for q in range(5):
        ftiles[5 + q % 3, :, pl.ds(q // 3 * 32, 32)] = fock_ref[2 * q:2 * q + 2, LANES:]

    @pl.loop(1, NR)
    def _(d):
        fock_copy((me + d) % NR).start()

    with jax.named_scope("tables"):
        for k in range(LAST + 1):
            rows = rows1(k, True)
            lands[k][pl.ds(me * R1 + FRONT, rows), :] = send1[pl.ds(me * S1 + CUTS[k] * SLOTS, rows), :]
        fgather[col, me] = ftiles[col]
        row = lax.broadcasted_iota(jnp.int32, (16, LANES), 0)
        two_early = (me == 1) | (me == 4) | (me == 11) | (me == 14)
        two_late = (me == 3) | (me == 12)
        is_pair = (row < 12) & ~((row // 2 == 3) & two_early) & ~((row // 2 == 5) & two_late)
        one = jnp.ones((16, LANES), jnp.float32)
        coef_a[0] = one
        coef_b[0] = jnp.zeros((16, LANES), jnp.float32)
        coef_a[1] = jnp.where(is_pair, 0.0, -one)
        coef_b[1] = jnp.where(is_pair, -one, 0.0)
        up_mask = (row % 2 == 0) & (row < 12)

        sub = lax.broadcasted_iota(jnp.int32, (8, LANES), 0)
        lane = lax.broadcasted_iota(jnp.int32, (8, LANES), 1)
        mine = ((sub % 2) * 8 + lane // NT - phase_ref[0, 0] + NR) % NR
        other = (mine + lane) % NT
        low = jnp.minimum(mine, other)
        high = jnp.maximum(mine, other)
        ident = low * NT - (low * (low - 1)) // 2 + (high - low)

        def look(d, at):
            for slot in range(SLOTS):
                block = jnp.where(slot < counts_ref[d], blocks_ref[d, slot], -1)
                at = jnp.where(ident == block, d * R1 + (FRONT + slot), at)
            return at

        at = lax.fori_loop(0, NR, look, jnp.full((8, LANES), FRONT, jnp.int32))
        vtable[...] = jnp.where(sub < 2, at, jnp.where(other > mine, 1, 0))
        to_smem = pltpu.make_async_copy(vtable, table, t_sem)
        to_smem.start()
        to_smem.wait()

    def pack2(k, to, dst, slot):
        first = CUTS[k]
        n = CUTS[k + 1] - first
        base = slot * P2 + base2(k)
        land = lands[k]
        for c in range(NT):
            at = table[to // 8, (to % 8) * NT + c]
            if c == 0:
                dst[pl.ds(base, heads_in(k)), :] = land[pl.ds(at, heads_in(k), stride=2 * SLOTS), :]
                continue
            kind = table[2 + to // 8, (to % 8) * NT + c]
            v = land[pl.ds(at, n, stride=SLOTS), :]
            up = land[pl.ds(at + SLOTS, n, stride=SLOTS), :]
            down = land[pl.ds(at - SLOTS, n, stride=SLOTS), :]
            swapped = jnp.where(up_mask[first:first + n], up, down)
            dst[pl.ds(base + heads_in(k) + c - 1, n, stride=OTHERS), :] = (
                coef_a[kind, first:first + n] * v + coef_b[kind, first:first + n] * swapped)

    for k in range(LAST + 1):
        with jax.named_scope(f"wait1_{k}"):
            at_size(k, long, lambda value: wait_rows(lands[k], OTHERS * rows1(k, value), r1_sem.at[k]))

        with jax.named_scope(f"pack2_{k}"):
            @pl.loop(1, NR)
            def _(d):
                to = (me + d) % NR
                pack2(k, to, send2, to)
                at_size(k, long, lambda value: send_2(k, to, rows2(k, value)).start())

            pack2(k, me, recv2, me)

    with jax.named_scope("waitf"):
        wait_rows(send1, OTHERS * 2, fr_sem)
        for d in range(1, NC):
            exchange(d).start()
        both(long, lambda value: wait_rows(
            send1,
            OTHERS * CUTS[LAST] * SLOTS + (8 - value) * rows1(LAST, True) + (7 + value) * rows1(LAST, False),
            s1_sem))

    def put(h, y, at, rows):
        target, column = (early, y) if y < EARLY else (dense, y - EARLY)
        target[h, column, at, :] = rows

    def assemble(k):
        for m in range(NR):
            for j, (x, y, h) in enumerate(pieces[m]):
                if not CUTS[k] <= j < CUTS[k + 1]:
                    continue
                i = j - CUTS[k]
                base = m * P2 + base2(k)
                rows = recv2[pl.ds(base + heads_in(k) + i * OTHERS, OTHERS), :]
                put(h, y, pl.ds(x + BT, OTHERS, stride=BT), rows)
                if x < y:
                    head = recv2[pl.ds(base + i // 2, 1), :]
                    put(h, y, pl.ds(x, 1), head)
                    put(h, x, pl.ds(y, 1), -head)
                elif x == y:
                    put(h, y, pl.ds(x, 1), jnp.zeros((1, LANES), jnp.float32))

    for k in range(LAST):
        with jax.named_scope(f"wait2_{k}"):
            wait_rows(recv2, OTHERS * rows2(k, True), r2_sem.at[k])

        with jax.named_scope(f"assemble_{k}"):
            assemble(k)

    with jax.named_scope("fock"):
        wait_rows(send1, (NC - 1) * 2 * NR, dr_sem)
        wait_rows(send1, (NC - 1) * 2 * NR, ds_sem)
        wait_rows(send1, OTHERS * 2, fs_sem)
        for d in range(NR):
            for q in range(5):
                at = pl.ds(d * BT + 2 * q, 2)
                ffull[at, :LANES] = fgather[q, d]
                ffull[at, LANES:] = fgather[5 + q % 3, d, :, pl.ds(q // 3 * 32, 32)]
        turn = (me - phase_ref[0, 0] + NR) % NR * BT
        size = NT * BT
        shifted = lax.broadcasted_iota(jnp.int32, (size, size), 1) + turn
        shifted = jnp.where(shifted >= size, shifted - size, shifted)
        picks = (lax.broadcasted_iota(jnp.int32, (size, size), 0) == shifted).astype(jnp.float32).astype(jnp.bfloat16)
        f = ffull[...]
        f_high = f.astype(jnp.bfloat16)
        f_low = (f - f_high.astype(jnp.float32)).astype(jnp.bfloat16)
        high_ref[...] = jnp.dot(f_high, picks, preferred_element_type=jnp.float32).astype(jnp.bfloat16)
        low_ref[...] = jnp.dot(f_low, picks, preferred_element_type=jnp.float32).astype(jnp.bfloat16)

    with jax.named_scope("matmul_0"):
        contract(high_ref, low_ref, early, range(EARLY), head_ref)

    with jax.named_scope(f"wait2_{LAST}"):
        both(long, lambda value: wait_rows(
            recv2, (8 - value) * rows2(LAST, True) + (7 + value) * rows2(LAST, False), r2_sem.at[LAST]))

    with jax.named_scope(f"assemble_{LAST}"):
        assemble(LAST)

    with jax.named_scope("drain"):
        both(long, lambda value: wait_rows(send2, OTHERS * sum(rows2(k, value) for k in range(LAST + 1)), s2_sem))


def finish(head_ref, dense, high_ref, low_ref, out_hbm, late, h_sem, o_sem):
    copies = [pltpu.make_async_copy(head_ref, out_hbm.at[0, pl.ds(0, EARLY)], h_sem)]
    copies[0].start()
    for y in range(BT - EARLY):
        contract(high_ref, low_ref, dense, (y,), late)
        copies.append(pltpu.make_async_copy(late.at[y], out_hbm.at[0, EARLY + y], o_sem.at[y]))
        copies[-1].start()
    for copy in copies:
        copy.wait()


def body(amplitudes, old_blocks, old_counts, new_phase, fock):
    nocc = amplitudes.shape[3]
    turned = jnp.transpose(amplitudes, (1, 2, 0, 3))
    phase = new_phase.reshape(1, 1)
    hbm = pl.BlockSpec(memory_space=pltpu.HBM)
    operands = [
        pltpu.with_memory_space_constraint(array, pltpu.HBM)
        for array in (old_blocks, old_counts, turned, fock)
    ]
    size = NT * BT
    vmem = pl.BlockSpec(memory_space=pltpu.VMEM)
    parts = pl.pallas_call(
        kernel,
        name="fock_two_phase",
        out_shape=(
            jax.ShapeDtypeStruct((EARLY, size, nocc), jnp.float32),
            jax.ShapeDtypeStruct((2, BT - EARLY, size, LANES), jnp.float32),
            jax.ShapeDtypeStruct((size, size), jnp.bfloat16),
            jax.ShapeDtypeStruct((size, size), jnp.bfloat16),
        ),
        in_specs=[pl.BlockSpec(memory_space=pl.ANY)] + [hbm] * 4,
        out_specs=(vmem,) * 4,
        scratch_shapes=[
            pltpu.SMEM(phase.shape, jnp.int32),
            pltpu.SMEM(old_blocks.shape, jnp.int32),
            pltpu.SMEM(old_counts.shape, jnp.int32),
            pltpu.VMEM(fock.shape, jnp.float32),
            pltpu.VMEM(turned.shape, jnp.float32),
            pltpu.VMEM((NR * S1, LANES), jnp.float32),
            pltpu.VMEM((NR * R1, LANES), jnp.float32),
            pltpu.VMEM((NR * R1, LANES), jnp.float32),
            pltpu.VMEM((NR * R1, LANES), jnp.float32),
            pltpu.VMEM((NR * P2, LANES), jnp.float32),
            pltpu.VMEM((NR * P2, LANES), jnp.float32),
            pltpu.VMEM((2, 16, LANES), jnp.float32),
            pltpu.VMEM((2, 16, LANES), jnp.float32),
            pltpu.VMEM((NC, 2, LANES), jnp.float32),
            pltpu.VMEM((NC, NR, 2, LANES), jnp.float32),
            pltpu.VMEM((size, size), jnp.float32),
            pltpu.VMEM((2, EARLY, size, LANES), jnp.float32),
            pltpu.VMEM((8, LANES), jnp.int32),
            pltpu.SMEM((8, LANES), jnp.int32),
        ] + [pltpu.SemaphoreType.DMA((3,))] + [pltpu.SemaphoreType.DMA] * 6 + [
            pltpu.SemaphoreType.DMA((3,)),
            pltpu.SemaphoreType.DMA,
            pltpu.SemaphoreType.DMA((3,)),
        ] + [pltpu.SemaphoreType.DMA] * 4,
        compiler_params=pltpu.CompilerParams(
            collective_id=0, has_side_effects=True, vmem_limit_bytes=48 << 20),
    )(phase, *operands)
    return pl.pallas_call(
        finish,
        name="fock_finish",
        out_shape=jax.ShapeDtypeStruct((1, BT, size, nocc), jnp.float32),
        in_specs=[vmem] * 4,
        out_specs=hbm,
        scratch_shapes=[
            pltpu.VMEM((BT - EARLY, size, nocc), jnp.float32),
            pltpu.SemaphoreType.DMA,
            pltpu.SemaphoreType.DMA((BT - EARLY,)),
        ],
        compiler_params=pltpu.CompilerParams(vmem_limit_bytes=16 << 20),
    )(*parts)


def solution(mesh):
    return jax.shard_map(
        body,
        mesh=mesh,
        in_specs=(P("row", None, None, "col"), P(), P(), P(), P("row", None)),
        out_specs=P("row", None, None, "col"),
        check_vma=False,
    )
```

time: 42.3 us -> 42.2 us (level)
  no operation moved by 1% of the time
where the time goes in v4:
time: 42.2 us; the launch traced here: 42.1 us
  Pallas kernels  41.4 us (98%)
  between operations  0.66 us (2%)
    pallas_call x1, Pallas kernels, body(): pl.pallas_call(kernel, name='fock_two_phase', out_shape=(jax.ShapeDtypeSt...  40.1 us
    pallas_call x1, Pallas kernels, body(): pl.pallas_call(finish, name='fock_finish', out_shape=jax.ShapeDtypeStruct...  1.33 us

profile of v4, /device:TPU:0, one launch (start us, length us, event | category | flops | bytes accessed | tf_op | source)
XLA Modules:
  0.0 42.1 jit_solution(5962490603660638598)
XLA Ops:
  0.7 40.1 %fock_two_phase.1 = (f32[4,160,256]{2,1,0:T(8,128)S(1)}, f32[2,6,160,128]{3,2,1,0:T(8,128)S(1)}, bf16[160,160]{1,0:T(8,128)(2,1)S(1)}, bf16[160,160]{1,0:T(8,128)(2,1)S(1)}) custom-call(s32[1,1]{1,0:T(1,128)} %bitcast.2.phase_hbm, s32[16,12]{1,0:T(8,128)} %blocks_hbm.1, s32[16]{0:T(128)} %counts_hbm.1, f32[10,10,12,256]{3,2,1,0:T(8,128)} %bitcast.3, ...), custom_call_target="tpu_custom_call" | custom-call | tf_op jit(solution)/shard_map/fock_two_phase/pallas_call | solution.py:372
  40.7 1.3 %fock_finish.1 = f32[1,10,160,256]{3,2,1,0:T(8,128)} custom-call(f32[4,160,256]{2,1,0:T(8,128)S(1)} %get-tuple-element.9.head_ref, f32[2,6,160,128]{3,2,1,0:T(8,128)S(1)} %get-tuple-element.10.dense, bf16[160,160]{1,0:T(8,128)(2,1)S(1)} %get-tuple-element.11.high_ref, bf16[160,160]{1,0:T(8,128)(2,1)S(1)} %get-tuple-element.12.low_ref), custom_call_target="tpu_custom_call" | custom-call | tf_op jit(solution)/shard_map/fock_finish/pallas_call | solution.py:411

commit v5 on v4

--- a/solution.py
+++ b/solution.py
@@ -22,15 +22,6 @@
 OTHERS = NT - 1
 CUTS = (0, 4, 8, 13)
 LAST = len(CUTS) - 2
-MESH = pl.DeviceIdType.MESH
-S1 = 160
-R1 = 96
-FRONT = 16
-LATE = 128
-OTHERS = NT - 1
-HEAD = (SPLIT // 2, 2)
-ROWS1 = SPLIT * SLOTS
-ROWS2 = SPLIT * OTHERS + HEAD[0]
 
 
 def is_long(m):
@@ -92,21 +83,18 @@
     pltpu.make_async_copy(part, part, sem).wait()
 
 
-def contract(high_ref, low_ref, dense, columns, out):
-    f_high = high_ref[...]
-    f_low = low_ref[...]
+def contract(f_ref, dense, columns, out):
+    f = f_ref[...]
     for y in columns:
         column = jnp.concatenate([dense[0, y], dense[1, y]], axis=1)
         c_high = column.astype(jnp.bfloat16)
         c_low = (column - c_high.astype(jnp.float32)).astype(jnp.bfloat16)
-        out[y] = (
-            jnp.dot(f_high, c_high, preferred_element_type=jnp.float32)
-            + jnp.dot(f_high, c_low, preferred_element_type=jnp.float32)
-            + jnp.dot(f_low, c_high, preferred_element_type=jnp.float32))
+        stack = jnp.concatenate([c_high, c_low, c_high], axis=0)
+        out[y] = jnp.dot(f, stack, preferred_element_type=jnp.float32)
 
 
 def kernel(
-    phase_hbm, blocks_hbm, counts_hbm, amp_hbm, fock_hbm, head_ref, dense, high_ref, low_ref,
+    phase_hbm, blocks_hbm, counts_hbm, amp_hbm, fock_hbm, head_ref, dense, f3_ref,
     phase_ref, blocks_ref, counts_ref, fock_ref, amp, send1, land0, land1, land2, send2, recv2, coef_a, coef_b,
     ftiles, fgather, ffull, early, vtable, table,
     a_sem, p_sem, b_sem, c_sem, f_sem, t_sem, s1_sem, r1_sem, s2_sem, r2_sem, fs_sem, fr_sem, ds_sem, dr_sem,
@@ -324,17 +312,21 @@
                 ffull[at, LANES:] = fgather[5 + q % 3, d, :, pl.ds(q // 3 * 32, 32)]
         turn = (me - phase_ref[0, 0] + NR) % NR * BT
         size = NT * BT
-        shifted = lax.broadcasted_iota(jnp.int32, (size, size), 1) + turn
+        wide = lax.broadcasted_iota(jnp.int32, (size, 3 * size), 1)
+        part = (wide >= size).astype(jnp.int32) + (wide >= 2 * size).astype(jnp.int32)
+        shifted = wide - part * size + turn
         shifted = jnp.where(shifted >= size, shifted - size, shifted)
-        picks = (lax.broadcasted_iota(jnp.int32, (size, size), 0) == shifted).astype(jnp.float32).astype(jnp.bfloat16)
+        picks = (lax.broadcasted_iota(jnp.int32, (size, 3 * size), 0) == shifted).astype(jnp.float32)
         f = ffull[...]
         f_high = f.astype(jnp.bfloat16)
         f_low = (f - f_high.astype(jnp.float32)).astype(jnp.bfloat16)
-        high_ref[...] = jnp.dot(f_high, picks, preferred_element_type=jnp.float32).astype(jnp.bfloat16)
-        low_ref[...] = jnp.dot(f_low, picks, preferred_element_type=jnp.float32).astype(jnp.bfloat16)
+        f3_ref[...] = (
+            jnp.dot(f_high, jnp.where(part < 2, picks, 0.0).astype(jnp.bfloat16), preferred_element_type=jnp.float32)
+            + jnp.dot(f_low, jnp.where(part == 2, picks, 0.0).astype(jnp.bfloat16), preferred_element_type=jnp.float32)
+        ).astype(jnp.bfloat16)
 
     with jax.named_scope("matmul_0"):
-        contract(high_ref, low_ref, early, range(EARLY), head_ref)
+        contract(f3_ref, early, range(EARLY), head_ref)
 
     with jax.named_scope(f"wait2_{LAST}"):
         both(long, lambda value: wait_rows(
@@ -347,11 +339,11 @@
         both(long, lambda value: wait_rows(send2, OTHERS * sum(rows2(k, value) for k in range(LAST + 1)), s2_sem))
 
 
-def finish(head_ref, dense, high_ref, low_ref, out_hbm, late, h_sem, o_sem):
+def finish(head_ref, dense, f3_ref, out_hbm, late, h_sem, o_sem):
     copies = [pltpu.make_async_copy(head_ref, out_hbm.at[0, pl.ds(0, EARLY)], h_sem)]
     copies[0].start()
     for y in range(BT - EARLY):
-        contract(high_ref, low_ref, dense, (y,), late)
+        contract(f3_ref, dense, (y,), late)
         copies.append(pltpu.make_async_copy(late.at[y], out_hbm.at[0, EARLY + y], o_sem.at[y]))
         copies[-1].start()
     for copy in copies:
@@ -375,11 +367,10 @@
         out_shape=(
             jax.ShapeDtypeStruct((EARLY, size, nocc), jnp.float32),
             jax.ShapeDtypeStruct((2, BT - EARLY, size, LANES), jnp.float32),
-            jax.ShapeDtypeStruct((size, size), jnp.bfloat16),
-            jax.ShapeDtypeStruct((size, size), jnp.bfloat16),
+            jax.ShapeDtypeStruct((size, 3 * size), jnp.bfloat16),
         ),
         in_specs=[pl.BlockSpec(memory_space=pl.ANY)] + [hbm] * 4,
-        out_specs=(vmem,) * 4,
+        out_specs=(vmem,) * 3,
         scratch_shapes=[
             pltpu.SMEM(phase.shape, jnp.int32),
             pltpu.SMEM(old_blocks.shape, jnp.int32),
@@ -412,7 +403,7 @@
         finish,
         name="fock_finish",
         out_shape=jax.ShapeDtypeStruct((1, BT, size, nocc), jnp.float32),
-        in_specs=[vmem] * 4,
+        in_specs=[vmem] * 3,
         out_specs=hbm,
         scratch_shapes=[
             pltpu.VMEM((BT - EARLY, size, nocc), jnp.float32),

time: 42.2 us -> 42.1 us (level)
  no operation moved by 1% of the time
where the time goes in v5:
time: 42.1 us; the launch traced here: 42 us
  Pallas kernels  41.3 us (98%)
  between operations  0.66 us (2%)
    pallas_call x1, Pallas kernels, body(): pl.pallas_call(kernel, name='fock_two_phase', out_shape=(jax.ShapeDtypeSt...  40.1 us
    pallas_call x1, Pallas kernels, body(): pl.pallas_call(finish, name='fock_finish', out_shape=jax.ShapeDtypeStruct...  1.25 us

profile of v5, /device:TPU:0, one launch (start us, length us, event | category | flops | bytes accessed | tf_op | source)
XLA Modules:
  0.0 42.0 jit_solution(12408624310109264478)
XLA Ops:
  0.7 40.1 %fock_two_phase.1 = (f32[4,160,256]{2,1,0:T(8,128)S(1)}, f32[2,6,160,128]{3,2,1,0:T(8,128)S(1)}, bf16[160,480]{1,0:T(8,128)(2,1)S(1)}) custom-call(s32[1,1]{1,0:T(1,128)} %bitcast.2.phase_hbm, s32[16,12]{1,0:T(8,128)} %blocks_hbm.1, s32[16]{0:T(128)} %counts_hbm.1, f32[10,10,12,256]{3,2,1,0:T(8,128)} %bitcast.3, f32[10,160]{1,0:T(8,128)} %fock_hbm.1), custom_call_target="tpu_custom_call" | custom-call | tf_op jit(solution)/shard_map/fock_two_phase/pallas_call | solution.py:364
  40.7 1.3 %fock_finish.1 = f32[1,10,160,256]{3,2,1,0:T(8,128)} custom-call(f32[4,160,256]{2,1,0:T(8,128)S(1)} %get-tuple-element.8.head_ref, f32[2,6,160,128]{3,2,1,0:T(8,128)S(1)} %get-tuple-element.9.dense, bf16[160,480]{1,0:T(8,128)(2,1)S(1)} %get-tuple-element.10.f3_ref), custom_call_target="tpu_custom_call" | custom-call | tf_op jit(solution)/shard_map/fock_finish/pallas_call | solution.py:402

commit v6 on v5

--- a/solution.py
+++ b/solution.py
@@ -104,6 +104,10 @@
     col = lax.axis_index("col")
     long = is_long(me)
     barrier = pltpu.get_barrier_semaphore()
+    for d in (10, 9, 11, 6, 14, 7, 5, 13, 15, 8, 2, 3, 12, 4, 1):
+        pl.semaphore_signal(barrier, inc=1, device_id={"row": (me + d) % NR}, device_id_type=MESH)
+    for d in range(1, NC):
+        pl.semaphore_signal(barrier, inc=1, device_id={"col": (col + d) % NC}, device_id_type=MESH)
     loads = [
         pltpu.make_async_copy(amp_hbm.at[part], amp.at[part], a_sem.at[i])
         for i, part in enumerate((
@@ -121,10 +125,7 @@
     ]
     for copy in small:
         copy.start()
-    for d in range(1, NR):
-        pl.semaphore_signal(barrier, inc=1, device_id={"row": (me + d) % NR}, device_id_type=MESH)
-    for d in range(1, NC):
-        pl.semaphore_signal(barrier, inc=1, device_id={"col": (col + d) % NC}, device_id_type=MESH)
+
     def pack1(first, last):
         for m in range(NR):
             for j, (x, y, h) in enumerate(pieces[m]):

time: 42.1 us -> 42.5 us (level); the launches traced: 42 us -> 41.7 us
  no operation moved by 1% of the time
where the time goes in v6:
time: 42.5 us; the launch traced here: 41.7 us
  Pallas kernels  41 us (96%)
  between operations  0.66 us (2%)
    pallas_call x1, Pallas kernels, body(): pl.pallas_call(kernel, name='fock_two_phase', out_shape=(jax.ShapeDtypeSt...  39.7 us
    pallas_call x1, Pallas kernels, body(): pl.pallas_call(finish, name='fock_finish', out_shape=jax.ShapeDtypeStruct...  1.26 us

profile of v6, /device:TPU:0, one launch (start us, length us, event | category | flops | bytes accessed | tf_op | source)
XLA Modules:
  0.0 41.7 jit_solution(13597976696528411324)
XLA Ops:
  0.7 39.7 %fock_two_phase.1 = (f32[4,160,256]{2,1,0:T(8,128)S(1)}, f32[2,6,160,128]{3,2,1,0:T(8,128)S(1)}, bf16[160,480]{1,0:T(8,128)(2,1)S(1)}) custom-call(s32[1,1]{1,0:T(1,128)} %bitcast.2.phase_hbm, s32[16,12]{1,0:T(8,128)} %blocks_hbm.1, s32[16]{0:T(128)} %counts_hbm.1, f32[10,10,12,256]{3,2,1,0:T(8,128)} %bitcast.3, f32[10,160]{1,0:T(8,128)} %fock_hbm.1), custom_call_target="tpu_custom_call" | custom-call | tf_op jit(solution)/shard_map/fock_two_phase/pallas_call | solution.py:365
  40.4 1.3 %fock_finish.1 = f32[1,10,160,256]{3,2,1,0:T(8,128)} custom-call(f32[4,160,256]{2,1,0:T(8,128)S(1)} %get-tuple-element.8.head_ref, f32[2,6,160,128]{3,2,1,0:T(8,128)S(1)} %get-tuple-element.9.dense, bf16[160,480]{1,0:T(8,128)(2,1)S(1)} %get-tuple-element.10.f3_ref), custom_call_target="tpu_custom_call" | custom-call | tf_op jit(solution)/shard_map/fock_finish/pallas_call | solution.py:403

commit v7 on v6

--- a/solution.py
+++ b/solution.py
@@ -104,7 +104,7 @@
     col = lax.axis_index("col")
     long = is_long(me)
     barrier = pltpu.get_barrier_semaphore()
-    for d in (10, 9, 11, 6, 14, 7, 5, 13, 15, 8, 2, 3, 12, 4, 1):
+    for d in range(1, NR):
         pl.semaphore_signal(barrier, inc=1, device_id={"row": (me + d) % NR}, device_id_type=MESH)
     for d in range(1, NC):
         pl.semaphore_signal(barrier, inc=1, device_id={"col": (col + d) % NC}, device_id_type=MESH)

time: 42.5 us -> 42.1 us (level); the launches traced: 41.7 us -> 42 us
  no operation moved by 1% of the time
where the time goes in v7:
time: 42.1 us; the launch traced here: 42 us
  Pallas kernels  41.3 us (98%)
  between operations  0.66 us (2%)
    pallas_call x1, Pallas kernels, body(): pl.pallas_call(kernel, name='fock_two_phase', out_shape=(jax.ShapeDtypeSt...  40.1 us
    pallas_call x1, Pallas kernels, body(): pl.pallas_call(finish, name='fock_finish', out_shape=jax.ShapeDtypeStruct...  1.25 us

profile of v7, /device:TPU:0, one launch (start us, length us, event | category | flops | bytes accessed | tf_op | source)
XLA Modules:
  0.0 42.0 jit_solution(10442160493545238830)
XLA Ops:
  0.7 40.1 %fock_two_phase.1 = (f32[4,160,256]{2,1,0:T(8,128)S(1)}, f32[2,6,160,128]{3,2,1,0:T(8,128)S(1)}, bf16[160,480]{1,0:T(8,128)(2,1)S(1)}) custom-call(s32[1,1]{1,0:T(1,128)} %bitcast.2.phase_hbm, s32[16,12]{1,0:T(8,128)} %blocks_hbm.1, s32[16]{0:T(128)} %counts_hbm.1, f32[10,10,12,256]{3,2,1,0:T(8,128)} %bitcast.3, f32[10,160]{1,0:T(8,128)} %fock_hbm.1), custom_call_target="tpu_custom_call" | custom-call | tf_op jit(solution)/shard_map/fock_two_phase/pallas_call | solution.py:365
  40.7 1.3 %fock_finish.1 = f32[1,10,160,256]{3,2,1,0:T(8,128)} custom-call(f32[4,160,256]{2,1,0:T(8,128)S(1)} %get-tuple-element.8.head_ref, f32[2,6,160,128]{3,2,1,0:T(8,128)S(1)} %get-tuple-element.9.dense, bf16[160,480]{1,0:T(8,128)(2,1)S(1)} %get-tuple-element.10.f3_ref), custom_call_target="tpu_custom_call" | custom-call | tf_op jit(solution)/shard_map/fock_finish/pallas_call | solution.py:403
